TPU v7x, 256 devices: a whole 4x4x8 slice. The times are simulated.
256 devices in a mesh: rows: 32 (over x, z), grp: 8 (over y, core).
Axes of the slice: x: 4, y: 4, z: 8, core: 2. Of those that a mesh axis runs over, the one named last changes fastest.
Arguments:
- matrix: float32 [524288, 1024], P(('rows', 'grp'))
- row_signs: int32 [524288], P(('rows', 'grp')), may hold values from -1 to 1, as said below
- samples: int32 [8192], P(('rows', 'grp')), may hold values from 0 to 524287, as said below
Outputs:
- factor: float32 [1024, 1024], P('rows')
Inputs may be any that keep to these rules, and one draw needn't show every extreme that they name: `row_signs`: every entry is 1 or -1. `samples`: entries are distinct and increasing; entries k * 32 to (k + 1) * 32 - 1 lie in rows k * 2048 to (k + 1) * 2048 - 1.
All inputs are finite; a program needn't handle non-finite values.
Results may differ from a plain program's by a relative error of at most 0.00011.
Values sent between devices are 32-bit elements; how exact they have to be, the bound alone decides.
No kernel may reach another device: no remote copies, remote signals or barrier semaphores. Data moves between devices by JAX's collectives and lax.ppermute only.
A program may use at most 128 MiB of HBM per device.

v0:
```python
import jax
import jax.numpy as jnp
import numpy as np
from jax import lax
from jax.sharding import Mesh
from jax.sharding import PartitionSpec as P

ROWS_GRP = ("rows_0", "rows_1", "grp_0", "grp_1")
ROWS = ("rows_0", "rows_1")
GRP = ("grp_0", "grp_1")


exact_mode = lax.Precision.HIGHEST


def in_blocks(array, dim, size):
    before, after = (array.shape[:dim], array.shape[dim + 1 :])
    return jnp.moveaxis(array.reshape(*before, size, -1, *after), dim, 0)


def summed_on_arrival(array, axis, dim):
    size = lax.axis_size(axis)
    pieces = lax.all_to_all(in_blocks(array, dim, size), axis, 0, 0, tiled=True)
    return jnp.sum(pieces, axis=0)


def sum_by_axis(array, axes, dim):
    far, near = axes
    pieces = in_blocks(array, dim, lax.axis_size(far))
    nearer = summed_on_arrival(pieces, near, dim + 1)
    arrived = lax.all_to_all(nearer, far, split_axis=0, concat_axis=0, tiled=True)
    return arrived.sum(axis=0)


def rows_for(lines, size):
    spare = -len(lines) % size
    return jnp.pad(lines, [(0, spare)] + [(0, 0)] * (lines.ndim - 1))


def sent_to_all(array, axis):
    size = lax.axis_size(axis)
    return lax.all_to_all(
        jnp.broadcast_to(array[None], (size, *array.shape)), axis, 0, 0, tiled=True
    )


def in_order(pieces, dim):
    pieces = jnp.moveaxis(pieces, 0, dim)
    lengths = pieces.shape
    return pieces.reshape(*lengths[:dim], lengths[dim] * lengths[dim + 1], *lengths[dim + 2 :])


def whole_of(array, axes, dim):
    far, near = axes
    pieces = sent_to_all(sent_to_all(array, far), near)
    return in_order(pieces.swapaxes(0, 1).reshape(-1, *array.shape), dim)


def total_of(array, axes):
    lines = array.reshape(-1)
    own = sum_by_axis(rows_for(lines, lax.axis_size(axes[0]) * lax.axis_size(axes[1])), axes, 0)
    whole = whole_of(own, axes, 0)
    return whole[: len(lines)].reshape(array.shape)


def joined_exchange(array, axis, axes, splits, concats):
    sizes = [lax.axis_size(a) for a in axes]
    pieces = in_blocks(array, splits[0], sizes[0])
    pieces = jnp.moveaxis(in_blocks(pieces, splits[1] + 1, sizes[1]), 0, 1)
    inside = pieces.shape[2:]
    pieces = pieces.reshape(-1, *inside)
    pieces = lax.all_to_all(pieces, axis, split_axis=0, concat_axis=0, tiled=True)
    pieces = in_order(pieces.reshape(*sizes, *inside), concats[0] + 1)
    return in_order(pieces, concats[1])


def parity_sign(left, right, length):
    correlation = left & right
    ones_total = jnp.zeros_like(correlation)
    for bit_level in range(max(1, length.bit_length() - 1)):
        ones_total = ones_total + (correlation >> bit_level & 1)
    return (1 - 2 * (ones_total % 2)).astype(jnp.float32)


def sylvester(length):
    indices = jnp.arange(length, dtype=jnp.int32)
    return parity_sign(indices[:, None], indices[None, :], length)


def upper_tiles_sum(local_gram):
    col_count = local_gram.shape[0]
    tile_width = col_count // 8
    first_tile = np.array([i for i in range(8) for j in range(i, 8)], dtype=np.int32)
    second_tile = np.array([j for i in range(8) for j in range(i, 8)], dtype=np.int32)
    tiled = local_gram.reshape(8, tile_width, 8, tile_width).transpose(0, 2, 1, 3)
    packed = tiled[first_tile, second_tile]
    summed = total_of(packed, (("rows_0", "rows_1"), ("grp_0", "grp_1")))
    placed = (
        jnp.zeros((8, 8, tile_width, tile_width), jnp.float32)
        .at[first_tile, second_tile]
        .set(summed)
    )
    mirrored = placed.transpose(1, 0, 3, 2)
    upper_place = np.arange(8)[:, None] <= np.arange(8)[None, :]
    whole = jnp.where(upper_place[:, :, None, None], placed, mirrored)
    return whole.transpose(0, 2, 1, 3).reshape(col_count, col_count)


def shards(matrix, row_signs, samples):
    count_rows = lax.axis_size(ROWS)
    count_grp = lax.axis_size(GRP)
    blocks = count_rows * count_grp
    row_dev, col_count = matrix.shape
    piece_rows = row_dev // blocks
    total_rows = row_dev * blocks
    sample_dev = samples.shape[0]
    position = lax.axis_index(ROWS_GRP)
    signed = matrix * row_signs.astype(jnp.float32)[:, None]
    before = jnp.dot(sylvester(row_dev), signed, precision=exact_mode)
    arrived = joined_exchange(
        before.reshape(1, 1, row_dev, col_count), ROWS_GRP, (ROWS, GRP), (2, 2), (0, 1)
    )
    mixed_rows = jnp.dot(
        sylvester(blocks), arrived.reshape(blocks, piece_rows * col_count), precision=exact_mode
    )
    mixed_rows = mixed_rows.reshape(count_rows, count_grp, piece_rows, col_count)
    mixed_rows = mixed_rows / jnp.sqrt(jnp.float32(total_rows))
    all_indices = whole_of(samples, (("rows_0", "rows_1"), ("grp_0", "grp_1")), 0)
    owner_block = all_indices // row_dev
    within = all_indices % row_dev - position * piece_rows
    owner_hit = (owner_block[:, None] == jnp.arange(blocks, dtype=jnp.int32)[None, :]).astype(
        jnp.float32
    )
    local_hit = (within[:, None] == jnp.arange(piece_rows, dtype=jnp.int32)[None, :]).astype(
        jnp.float32
    )
    weights = jnp.einsum("kb,kt->bt", owner_hit, local_hit, precision=exact_mode).reshape(
        blocks * piece_rows
    )
    flat_rows = mixed_rows.reshape(blocks * piece_rows, col_count)
    local_gram = jnp.einsum(
        "kn,km->nm", flat_rows * weights[:, None], flat_rows, precision=exact_mode
    )
    summed_gram = upper_tiles_sum(local_gram)
    gram_total = summed_gram * (total_rows / (sample_dev * blocks))
    lower_factor = jnp.linalg.cholesky(gram_total)
    upper_factor = lower_factor.T
    share_rows = col_count // count_rows
    return lax.dynamic_slice_in_dim(upper_factor, lax.axis_index(ROWS) * share_rows, share_rows, 0)


def solution(mesh):
    finer = Mesh(mesh.devices.reshape(4, 8, 4, 2), ("rows_0", "rows_1", "grp_0", "grp_1"))
    return jax.shard_map(
        shards,
        mesh=finer,
        in_specs=(P(ROWS_GRP, None), P(ROWS_GRP), P(ROWS_GRP)),
        out_specs=P(ROWS, None),
        check_vma=False,
    )
```

profile of v0, /device:TPU:1, one launch (start us, length us, event | category | flops | bytes accessed | tf_op | source)
XLA Modules:
  0.0 778.4 jit_solution(3198407191424926384)
XLA Ops:
  1.3 11.9 %all-to-all-start.1 = ((s32[32,1,32]{2,1,0:T(1,128)}), s32[32,1,32]{2,1,0:T(1,128)S(1)}, u32[]{:S(2)}, u32[]{:S(2)}) async-start(s32[32,1,32]{2,1,0:T(1,128)} %broadcast_in_dim.69), calls=%async_computation.1 | async-start | bytes 32768 | tf_op jit(solution)/shard_map/all_to_all | solution.py:42
  29.0 83.9 %fusion.29 = f32[256,1,1,8,1024]{4,3,2,1,0:T(8,128)} fusion(f32[2048,1024]{1,0:T(8,128)} %fusion.114), kind=kOutput, calls=%fused_computation.38 | convolution fusion | flops 51736739840 | bytes 16777216 | tf_op jit(solution)/shard_map/dot_general | solution.py:119
  113.0 12.1 %all-to-all-start = ((f32[256,1,1,8,1024]{4,3,2,1,0:T(8,128)}), f32[256,1,1,8,1024]{4,3,2,1,0:T(8,128)}, u32[]{:S(2)}, u32[]{:S(2)}) async-start(f32[256,1,1,8,1024]{4,3,2,1,0:T(8,128)} %fusion.29), calls=%async_computation | async-start | bytes 16777216 | tf_op jit(solution)/shard_map/all_to_all | solution.py:72
  129.3 183.0 %all-to-all-done = f32[256,1,1,8,1024]{4,3,2,1,0:T(8,128)} async-done(((f32[256,1,1,8,1024]{4,3,2,1,0:T(8,128)}), f32[256,1,1,8,1024]{4,3,2,1,0:T(8,128)}, u32[]{:S(2)}, u32[]{:S(2)}) %all-to-all-start) | async-done | bytes 8388640 | tf_op jit(solution)/shard_map/all_to_all | solution.py:72
  312.3 15.0 %copy.90 = f32[32,8,8,1024]{3,1,2,0:T(8,128)} copy(f32[32,8,8,1024]{3,2,1,0:T(8,128)} %bitcast.56) | data formatting | bytes 16777216
  327.3 9.0 %copy.59 = f32[8192,256]{1,0:T(8,128)} copy(f32[8192,256]{0,1:T(8,128)} %bitcast.119) | data formatting | bytes 16777216 | tf_op jit(solution)/shard_map/dot_general | solution.py:123
  336.3 11.3 %broadcast_multiply_fusion = f32[32,8,8,1024]{3,1,2,0:T(8,128)S(1)} fusion(f32[8,1024,256,1]{2,1,0,3:T(8,128)} %bitcast.118, s32[32,8]{1,0:T(8,128)S(1)} %multiply_add_fusion), kind=kOutput, calls=%fused_computation.36 | convolution fusion | flops 6447038464 | bytes 16778240 | tf_op jit(solution)/shard_map/dot_general | solution.py:123
  347.6 8.4 %copy.60 = f32[32,8,8,1024]{3,2,1,0:T(8,128)S(1)} copy(f32[32,8,8,1024]{3,1,2,0:T(8,128)S(1)} %broadcast_multiply_fusion) | data formatting | bytes 16777216 | tf_op jit(solution)/shard_map/div | solution.py:127
  361.8 9.1 %copy.87 = f32[1024,2048]{1,0:T(8,128)} copy(f32[1024,2048]{0,1:T(8,128)} %bitcast.120) | data formatting | bytes 16777216 | tf_op jit(solution)/shard_map/kn,km->nm/dot_general | solution.py:141
  371.0 9.1 %copy.88 = f32[1024,2048]{1,0:T(8,128)} copy(f32[1024,2048]{0,1:T(8,128)} %bitcast.115) | data formatting | bytes 16777216 | tf_op jit(solution)/shard_map/kn,km->nm/dot_general | solution.py:141
  380.1 33.1 %convolution_bitcast_fusion = f32[8,8,128,128]{3,2,1,0:T(8,128)} fusion(f32[8,128,2048,1]{2,1,3,0:T(8,128)} %bitcast.124, f32[8,128,2048,1]{2,1,0,3:T(8,128)} %bitcast.125), kind=kOutput, calls=%fused_computation.40 | convolution fusion | flops 25769803776 | bytes 20971520 | tf_op jit(solution)/shard_map/kn,km->nm/dot_general | solution.py:141
  420.2 33.9 %all_to_all.41 = f32[8,32,2304]{2,1,0:T(8,128)S(1)} all-to-all(f32[8,32,2304]{2,1,0:T(8,128)S(1)} %bitcast.123), channel_id=1, replica_groups=mesh['rows_0'=4,'rows_1'=8,'grp_0'=4,'grp_1'=2] {'grp_0','grp_1'}, dimensions={0} | all-to-all | bytes 4718592 | tf_op jit(solution)/shard_map/all_to_all | solution.py:23
  454.4 12.9 %all_to_all.42 = f32[32,1,2304]{2,1,0:T(1,128)S(1)} all-to-all(f32[32,1,2304]{2,1,0:T(1,128)S(1)} %all_to_all.30), channel_id=1, replica_groups=mesh['rows_0'=4,'rows_1'=8,'grp_0'=4,'grp_1'=2] {'rows_0','rows_1'}, dimensions={0} | all-to-all | bytes 589824 | tf_op jit(solution)/shard_map/all_to_all | solution.py:31
  467.7 16.2 %all_to_all.43 = f32[32,1,2304]{2,1,0:T(1,128)S(1)} all-to-all(f32[32,1,2304]{2,1,0:T(1,128)S(1)} %broadcast_in_dim.74), channel_id=1, replica_groups=mesh['rows_0'=4,'rows_1'=8,'grp_0'=4,'grp_1'=2] {'rows_0','rows_1'}, dimensions={0} | all-to-all | bytes 589824 | tf_op jit(solution)/shard_map/all_to_all | solution.py:42
  485.5 7.5 all-to-all-start.6
  493.0 29.0 %all-to-all-done.6 = f32[8,32,2304]{2,1,0:T(8,128)S(1)} async-done(((f32[8,32,2304]{2,1,0:T(8,128)}), f32[8,32,2304]{2,1,0:T(8,128)S(1)}, u32[]{:S(2)}, u32[]{:S(2)}) %all-to-all-start.6) | async-done | bytes 2359328 | tf_op jit(solution)/shard_map/all_to_all | solution.py:42
  529.6 8.4 %scatter_fusion = f32[8,8,128,128]{3,2,1,0:T(8,128)} fusion(f32[8,8,128,128]{3,2,1,0:T(8,128)} %broadcast_in_dim.32, s32[36]{0:T(128)S(1)} %copy-done.2, f32[36,128,128]{2,1,0:T(8,128)S(1)} %reshape.293), kind=kCustom, calls=%fused_computation.1 | custom fusion | bytes 7078176 | tf_op jit(solution)/shard_map/scatter | solution.py:101
  572.3 11.7 %cholesky.223 = f32[128,128]{1,0:T(8,128)S(1)} custom-call(f32[128,128]{1,0:T(8,128)S(1)} %cholesky.580), custom_call_target="Cholesky" | custom-call | tf_op jit(solution)/shard_map/jit(cholesky)/cholesky | solution.py:146
  586.5 9.8 %custom-call.59 = f32[1,128,128]{1,2,0:T(8,128)S(1)} custom-call(f32[1,128,128]{2,1,0:T(8,128)S(1)} %get-tuple-element.26), custom_call_target="InvertDiagBlocksLowerTriangular" | custom-call | tf_op jit(solution)/shard_map/jit(cholesky)/cholesky | solution.py:146
  600.1 11.9 %cholesky.244 = f32[128,128]{1,0:T(8,128)S(1)} custom-call(f32[128,128]{1,0:T(8,128)S(1)} %cholesky.584), custom_call_target="Cholesky" | custom-call | tf_op jit(solution)/shard_map/jit(cholesky)/cholesky | solution.py:146
  613.5 9.8 %custom-call.60 = f32[1,128,128]{1,2,0:T(8,128)S(1)} custom-call(f32[1,128,128]{2,1,0:T(8,128)S(1)} %get-tuple-element.23), custom_call_target="InvertDiagBlocksLowerTriangular" | custom-call | tf_op jit(solution)/shard_map/jit(cholesky)/cholesky | solution.py:146
  626.7 11.7 %cholesky.468 = f32[128,128]{1,0:T(8,128)S(1)} custom-call(f32[128,128]{1,0:T(8,128)S(1)} %cholesky.589), custom_call_target="Cholesky" | custom-call | tf_op jit(solution)/shard_map/jit(cholesky)/cholesky | solution.py:146
  639.7 9.8 %custom-call.61 = f32[1,128,128]{1,2,0:T(8,128)S(1)} custom-call(f32[1,128,128]{2,1,0:T(8,128)S(1)} %get-tuple-element.20), custom_call_target="InvertDiagBlocksLowerTriangular" | custom-call | tf_op jit(solution)/shard_map/jit(cholesky)/cholesky | solution.py:146
  653.4 11.7 %cholesky.487 = f32[128,128]{1,0:T(8,128)S(1)} custom-call(f32[128,128]{1,0:T(8,128)S(1)} %cholesky.594), custom_call_target="Cholesky" | custom-call | tf_op jit(solution)/shard_map/jit(cholesky)/cholesky | solution.py:146
  666.4 9.8 %custom-call.62 = f32[1,128,128]{1,2,0:T(8,128)S(1)} custom-call(f32[1,128,128]{2,1,0:T(8,128)S(1)} %get-tuple-element.17), custom_call_target="InvertDiagBlocksLowerTriangular" | custom-call | tf_op jit(solution)/shard_map/jit(cholesky)/cholesky | solution.py:146
  679.7 11.7 %cholesky.506 = f32[128,128]{1,0:T(8,128)S(1)} custom-call(f32[128,128]{1,0:T(8,128)S(1)} %cholesky.599), custom_call_target="Cholesky" | custom-call | tf_op jit(solution)/shard_map/jit(cholesky)/cholesky | solution.py:146
  692.7 9.9 %custom-call.63 = f32[1,128,128]{1,2,0:T(8,128)S(1)} custom-call(f32[1,128,128]{2,1,0:T(8,128)S(1)} %get-tuple-element.14), custom_call_target="InvertDiagBlocksLowerTriangular" | custom-call | tf_op jit(solution)/shard_map/jit(cholesky)/cholesky | solution.py:146
  706.0 11.7 %cholesky.526 = f32[128,128]{1,0:T(8,128)S(1)} custom-call(f32[128,128]{1,0:T(8,128)S(1)} %cholesky.604), custom_call_target="Cholesky" | custom-call | tf_op jit(solution)/shard_map/jit(cholesky)/cholesky | solution.py:146
  719.0 9.8 %custom-call.64 = f32[1,128,128]{1,2,0:T(8,128)S(1)} custom-call(f32[1,128,128]{2,1,0:T(8,128)S(1)} %get-tuple-element.11), custom_call_target="InvertDiagBlocksLowerTriangular" | custom-call | tf_op jit(solution)/shard_map/jit(cholesky)/cholesky | solution.py:146
  731.8 11.9 %cholesky.546 = f32[128,128]{1,0:T(8,128)S(1)} custom-call(f32[128,128]{1,0:T(8,128)S(1)} %cholesky.609), custom_call_target="Cholesky" | custom-call | tf_op jit(solution)/shard_map/jit(cholesky)/cholesky | solution.py:146
  744.9 9.8 %custom-call.65 = f32[1,128,128]{1,2,0:T(8,128)S(1)} custom-call(f32[1,128,128]{2,1,0:T(8,128)S(1)} %get-tuple-element.8), custom_call_target="InvertDiagBlocksLowerTriangular" | custom-call | tf_op jit(solution)/shard_map/jit(cholesky)/cholesky | solution.py:146
  757.3 11.7 %cholesky.564 = f32[128,128]{1,0:T(8,128)S(1)} custom-call(f32[128,128]{1,0:T(8,128)S(1)} %convolution_subtract_fusion.6), custom_call_target="Cholesky" | custom-call | tf_op jit(solution)/shard_map/jit(cholesky)/cholesky | solution.py:146
  (85 shorter events, 115.9 us)
Async XLA Ops:
  1.3 20.5 %all-to-all-start.1 = ((s32[32,1,32]{2,1,0:T(1,128)}), s32[32,1,32]{2,1,0:T(1,128)S(1)}, u32[]{:S(2)}, u32[]{:S(2)}) async-start(s32[32,1,32]{2,1,0:T(1,128)} %broadcast_in_dim.69), calls=%async_computation.1 | async-start | bytes 32768 | tf_op jit(solution)/shard_map/all_to_all | solution.py:42
  22.5 90.5 %all-to-all-start.2 = ((s32[8,1,1024]{2,1,0:T(1,128)}), s32[8,1,1024]{2,1,0:T(1,128)S(1)}, u32[]{:S(2)}, u32[]{:S(2)}) async-start(s32[8,1,1024]{2,1,0:T(1,128)} %reshape.301), calls=%async_computation.2 | async-start | bytes 65536 | tf_op jit(solution)/shard_map/all_to_all | solution.py:42
  113.0 199.3 %all-to-all-start = ((f32[256,1,1,8,1024]{4,3,2,1,0:T(8,128)}), f32[256,1,1,8,1024]{4,3,2,1,0:T(8,128)}, u32[]{:S(2)}, u32[]{:S(2)}) async-start(f32[256,1,1,8,1024]{4,3,2,1,0:T(8,128)} %fusion.29), calls=%async_computation | async-start | bytes 16777216 | tf_op jit(solution)/shard_map/all_to_all | solution.py:72
  356.1 5.8 copy-start
  380.1 33.1 %copy-start.2 = (s32[36]{0:T(128)S(1)}, s32[36]{0:T(128)}, u32[]{:S(2)}) copy-start(s32[36]{0:T(128)} %constant.436) | copy-start | bytes 436
  485.5 36.5 %all-to-all-start.6 = ((f32[8,32,2304]{2,1,0:T(8,128)}), f32[8,32,2304]{2,1,0:T(8,128)S(1)}, u32[]{:S(2)}, u32[]{:S(2)}) async-start(f32[8,32,2304]{2,1,0:T(8,128)} %broadcast_in_dim.76), calls=%async_computation.6 | async-start | bytes 4718592 | tf_op jit(solution)/shard_map/all_to_all | solution.py:42
  538.0 5.4 copy-start.3
  570.3 1.9 copy-start.1
where the time goes:
time: 793 us; the launch traced here: 778 us
  waiting for transfers between devices  213 us (27%)
  other arithmetic  197 us (25%)
  matrix products  154 us (19%)
  local copies, waits for them, and re-layouts  108 us (14%)
  blocking collectives  63 us (8%)
  starting transfers between devices  38 us (5%)
    all_to_all x1, waiting for transfers between devices, joined_exchange(): lax.all_to_all(pieces, axis, split_axis=0, concat_axis=0, tiled=True)  183 us
    another operation x30, other arithmetic, shards(): lower_factor = jnp.linalg.cholesky(gram_total)  172 us
    dot_general x1, matrix products, shards(): before = jnp.dot(sylvester(row_dev), signed, precision=exact_mode)  83.9 us
    all_to_all x1, blocking collectives, summed_on_arrival(): pieces = lax.all_to_all(in_blocks(array, dim, size), axis, 0, 0, tiled=True)  33.9 us
    dot_general x1, matrix products, shards(): jnp.einsum('kn,km->nm', flat_rows * weights[:, None], flat_rows, precisio...  33.1 us
    all_to_all x3, waiting for transfers between devices, sent_to_all(): lax.all_to_all(jnp.broadcast_to(array[None], (size, *array.shape)), axis,...  29.7 us
    all_to_all x3, starting transfers between devices, sent_to_all(): lax.all_to_all(jnp.broadcast_to(array[None], (size, *array.shape)), axis,...  25.9 us
    unnamed x13, local copies, waits for them, and re-layouts  24.5 us
  transfers between devices with their start and end apart: 4, of which 3 were waited for; matrix products, arithmetic and copies ran while one was open for 12% of the time, Pallas kernels for 0%

commit v1 on v0

v1 whole, which is shorter than its diff:
```python
import functools

import jax
import jax.numpy as jnp
from jax import lax
from jax.experimental import pallas as pl
from jax.experimental.pallas import tpu as pltpu
from jax.sharding import Mesh
from jax.sharding import PartitionSpec as P

ALL = ("x", "z", "y", "c")
PLANE = ("y", "c", "x")
EXACT = lax.Precision.HIGHEST
F32 = jnp.float32
BF16 = jnp.bfloat16
COLS = 1024
BLOCKS = 256
TILE = 128


def vmem(limit=100):
    return pltpu.CompilerParams(vmem_limit_bytes=limit * 1024 * 1024 // 2)


def turn_kernel(sign_ref, in_ref, out_ref):
    for t in range(in_ref.shape[0] // TILE):
        rows = slice(t * TILE, (t + 1) * TILE)
        sign = sign_ref[t : t + 1, :].astype(F32)
        out_ref[:, rows] = in_ref[rows, :].T * sign


def turned(matrix, row_signs):
    rows, cols = matrix.shape
    signs = row_signs.reshape(rows // TILE, TILE)
    return pl.pallas_call(
        turn_kernel,
        grid=(cols // TILE,),
        in_specs=[
            pl.BlockSpec(signs.shape, lambda i: (0, 0)),
            pl.BlockSpec((rows, TILE), lambda i: (0, i)),
        ],
        out_specs=pl.BlockSpec((TILE, rows), lambda i: (i, 0)),
        out_shape=jax.ShapeDtypeStruct((cols, rows), F32),
        compiler_params=vmem(),
        name="turn",
    )(signs, matrix)


def odd_ones(bits, count):
    for shift in (8, 4, 2, 1):
        if shift < count:
            bits = bits ^ (bits >> shift)
    return bits & 1


def signs_kernel(z_ref, sample_ref, low_ref, high_ref):
    block = pl.program_id(0)
    within = sample_ref[pl.ds(block, 1), :] & 2047
    wl = lax.broadcasted_iota(jnp.int32, (256, 256), 0)
    low = odd_ones(wl & (within & 255), 8)
    low_ref[0] = (1 - 2 * low).astype(F32).astype(BF16)
    wh = lax.broadcasted_iota(jnp.int32, (8, 256), 0)
    lane = lax.broadcasted_iota(jnp.int32, (8, 256), 1)
    odd = odd_ones(wh & (within >> 8), 4) ^ odd_ones((lane >> 5) & z_ref[0], 4)
    high_ref[0] = (1 - 2 * odd).astype(F32) * (2.0**-7)


def sampled_signs(z_index, samples):
    return pl.pallas_call(
        signs_kernel,
        grid=(32,),
        in_specs=[
            pl.BlockSpec(memory_space=pltpu.SMEM),
            pl.BlockSpec((32, 256), lambda i: (0, 0)),
        ],
        out_specs=[
            pl.BlockSpec((1, 256, 256), lambda i: (i, 0, 0)),
            pl.BlockSpec((1, 8, 256), lambda i: (i, 0, 0)),
        ],
        out_shape=[
            jax.ShapeDtypeStruct((32, 256, 256), BF16),
            jax.ShapeDtypeStruct((32, 8, 256), F32),
        ],
        compiler_params=vmem(),
        name="signs",
    )(z_index, samples)


def butterflies(values):
    span = 1
    while span < len(values):
        new = list(values)
        for i in range(len(values)):
            if not i & span:
                new[i] = values[i] + values[i + span]
                new[i + span] = values[i] - values[i + span]
        values = new
        span *= 2
    return values


def pick_kernel(in_ref, low_ref, high_ref, out_ref, parts_ref):
    wh = pl.program_id(0)

    @pl.when(wh == 0)
    def _():
        out_ref[...] = jnp.zeros_like(out_ref)

    for row in range(0, 32, 16):
        for lane in range(0, 256, TILE):
            lanes = slice(lane, lane + TILE)
            values = butterflies([in_ref[p, row : row + 16, lanes] for p in range(32)])
            for p in range(32):
                rest = values[p]
                for part in range(3):
                    piece = rest.astype(BF16)
                    parts_ref[p, 32 * part + row : 32 * part + row + 16, lanes] = piece
                    if part < 2:
                        rest = rest - piece.astype(F32)

    def one(p, carry):
        got = jnp.dot(parts_ref[p], low_ref[p], preferred_element_type=F32)
        got = got[0:32] + got[32:64] + got[64:96]
        out_ref[p] = out_ref[p] + got * high_ref[p, pl.ds(wh, 1), :]
        return carry

    lax.fori_loop(0, 32, one, 0, unroll=4)


def picked(blocks, low, high):
    return pl.pallas_call(
        pick_kernel,
        grid=(8,),
        in_specs=[
            pl.BlockSpec((32, 32, 256), lambda i: (0, 0, i)),
            pl.BlockSpec((32, 256, 256), lambda i: (0, 0, 0)),
            pl.BlockSpec((32, 8, 256), lambda i: (0, 0, 0)),
        ],
        out_specs=pl.BlockSpec((32, 32, 256), lambda i: (0, 0, 0)),
        out_shape=jax.ShapeDtypeStruct((32, 32, 256), F32),
        scratch_shapes=[pltpu.VMEM((32, 96, 256), BF16)],
        compiler_params=vmem(),
        name="pick",
    )(blocks, low, high)


def gram_kernel(own_ref, near_ref, far_ref, o_own_ref, o_near_ref, o_far_ref, out_ref):
    others = (own_ref, o_own_ref, near_ref, o_near_ref, far_ref, o_far_ref)
    for tile, other in enumerate(others):
        out_ref[tile] = lax.dot_general(
            own_ref[...],
            other[...],
            (((1,), (1,)), ((), ())),
            precision=EXACT,
            preferred_element_type=F32,
        )


def gram_tiles(*blocks):
    return pl.pallas_call(
        gram_kernel,
        out_shape=jax.ShapeDtypeStruct((6, TILE, TILE), F32),
        compiler_params=vmem(),
        name="gram",
    )(*blocks)


def over_lanes(block, lane):
    return jnp.broadcast_to(block[:, lane : lane + 1], (8, TILE))


def over_rows(block, row):
    return jnp.broadcast_to(block[row : row + 1, :], (8, TILE))


def inverse_root(d):
    root = lax.rsqrt(d)
    return root * (1.5 - 0.5 * (d * root) * root)


def factor_kernel(at_ref, *refs):
    tile_refs = refs[:8]
    out_ref, work, left = refs[8:]
    y, c, row0 = at_ref[0], at_ref[1], at_ref[2]
    for n, ref in enumerate(tile_refs):
        shift, other = n % 4, n // 4
        ys, cs = (y + shift) % 4, c ^ other
        a = 2 * ys + cs
        for tile in range(ref.shape[0]):
            dy, dc = tile // 2, tile % 2
            b = 2 * ((ys + dy) % 4) + (cs ^ dc)

            @pl.when(a <= b)
            def _(ref=ref, tile=tile, a=a, b=b):
                work[b, pl.ds(pl.multiple_of(a * TILE, TILE), TILE), :] = ref[tile] * 2.0

            @pl.when(a > b)
            def _(ref=ref, tile=tile, a=a, b=b):
                work[a, pl.ds(pl.multiple_of(b * TILE, TILE), TILE), :] = ref[tile].T * 2.0

    row_of = lax.broadcasted_iota(jnp.int32, (8, TILE), 0)

    def one_block(j, carry):
        base = j * TILE

        def rows(i):
            return pl.ds(pl.multiple_of(base + 8 * i, 8), 8)

        for t in range(16):
            head = work[j, rows(t), :]
            columns = [over_lanes(head, 8 * t + m) for m in range(8)]
            roots, lefts, pairs = [], [], {}
            scale = jnp.zeros((8, TILE), F32)
            for m in range(8):
                root = inverse_root(over_rows(columns[m], m))
                column = columns[m] * root
                for q in range(m + 1, 8):
                    pairs[q, m] = over_rows(column, q)
                    columns[q] = columns[q] - column * pairs[q, m]
                roots.append(root)
                lefts.append(jnp.where(row_of > m, column, 0.0))
                scale = jnp.where(row_of == m, root, scale)
            for i in range(t + 1, 16):
                block = work[j, rows(i), :]
                got = []
                for m in range(8):
                    value = over_lanes(block, 8 * t + m)
                    for q in range(m):
                        value = value - got[q] * pairs[m, q]
                    got.append(value * roots[m])
                    left[i, m] = got[m]

            def one_tile(k, carry, t=t, lefts=lefts, roots=roots, scale=scale):
                head = work[k, rows(t), :]
                for m in range(8):
                    head = head - lefts[m] * (over_rows(head, m) * roots[m])
                head = head * scale
                work[k, rows(t), :] = head
                if t < 15:
                    lines = [over_rows(head, m) for m in range(8)]
                    for i in range(t + 1, 16):
                        block = work[k, rows(i), :]
                        for m in range(8):
                            block = block - left[i, m] * lines[m]
                        work[k, rows(i), :] = block
                return carry

            lax.fori_loop(j, 8, one_tile, 0)

        for done in range(7):

            @pl.when(j == done)
            def _(done=done):
                rows_done = slice(done * TILE, (done + 1) * TILE)
                for i in range(done + 1, 8):
                    turned_tile = work[i, rows_done, :].T
                    for k in range(i, 8):
                        into = slice(i * TILE, (i + 1) * TILE)
                        work[k, into, :] = work[k, into, :] - jnp.dot(
                            turned_tile,
                            work[k, rows_done, :],
                            precision=EXACT,
                            preferred_element_type=F32,
                        )

        return carry

    lax.fori_loop(0, 8, one_block, 0)
    count = out_ref.shape[0]
    row = row0 + lax.broadcasted_iota(jnp.int32, (count, TILE), 0)
    for k in range(8):
        col = k * TILE + lax.broadcasted_iota(jnp.int32, (count, TILE), 1)
        mine = work[k, pl.ds(pl.multiple_of(row0, count), count), :]
        out_ref[:, k * TILE : (k + 1) * TILE] = jnp.where(col >= row, mine, 0.0)


def factored(at, tiles, share):
    return pl.pallas_call(
        factor_kernel,
        in_specs=[pl.BlockSpec(memory_space=pltpu.SMEM)]
        + [pl.BlockSpec(memory_space=pltpu.VMEM)] * len(tiles),
        out_specs=pl.BlockSpec(memory_space=pltpu.VMEM),
        out_shape=jax.ShapeDtypeStruct((share, COLS), F32),
        scratch_shapes=[
            pltpu.VMEM((8, COLS, TILE), F32),
            pltpu.VMEM((16, 8, 8, TILE), F32),
        ],
        compiler_params=vmem(),
        name="factor",
    )(at, *tiles)


def from_ahead(array, axis, shift):
    size = lax.axis_size(axis)
    return lax.ppermute(array, axis, [((i + shift) % size, i) for i in range(size)])


def in_line(array, axis):
    size = lax.axis_size(axis)
    near = [array] + [from_ahead(array, axis, s) for s in range(1, size)]
    twice = jnp.stack(near + near)
    return lax.dynamic_slice_in_dim(twice, size - lax.axis_index(axis), size, 0)


def all_samples(samples):
    lines = samples
    for axis in ("c", "y", "x", "z"):
        lines = in_line(lines, axis)
    return lines.transpose(2, 3, 1, 0, 4).reshape(32, -1)


def shards(matrix, row_signs, samples):
    rows, cols = matrix.shape
    at_y, at_c = lax.axis_index("y"), lax.axis_index("c")
    at_z, at_x = lax.axis_index("z"), lax.axis_index("x")
    flat = turned(matrix, row_signs)
    blocks = lax.all_to_all(flat.reshape(32, 32, rows), PLANE, 0, 0, tiled=True)
    low, high = sampled_signs(at_z.reshape(1), all_samples(samples))
    ours = picked(blocks, low, high)
    arrived = lax.all_to_all(ours, ("z", "x"), 0, 0, tiled=True)
    own = arrived.reshape(8, TILE, 256).sum(axis=0)
    near, far = from_ahead(own, "y", 1), from_ahead(own, "y", 2)
    others = [from_ahead(a, "c", 1) for a in (own, near, far)]
    tiles = gram_tiles(own, near, far, *others).reshape(32, 24, TILE)
    share = lax.all_to_all(tiles, ("z", "x"), 0, 0, tiled=True).sum(axis=0)
    whole = jnp.broadcast_to(share[None], (32, 24, TILE))
    whole = lax.all_to_all(whole, ("z", "x"), 0, 0, tiled=True).reshape(6, TILE, TILE)
    lines = [whole, from_ahead(whole, "y", 1)]
    lines += [from_ahead(whole[:4], "y", 2), from_ahead(whole[:4], "y", 3)]
    lines += [from_ahead(a, "c", 1) for a in lines]
    out_rows = COLS // 32
    at = jnp.stack([at_y, at_c, (at_x * 8 + at_z) * out_rows]).astype(jnp.int32)
    return factored(at, lines, out_rows)


def solution(mesh):
    finer = Mesh(mesh.devices.reshape(4, 8, 4, 2), ALL)
    return jax.shard_map(
        shards,
        mesh=finer,
        in_specs=(P(ALL, None), P(ALL), P(ALL)),
        out_specs=P(("x", "z"), None),
        check_vma=False,
    )
```

time: 793 us -> 348 us (0.44); the launches traced: 778 us -> 347 us
  other arithmetic: 197 us -> 0.19 us
  matrix products: 154 us -> 0 us
  Pallas kernels: 0 us -> 119 us
  waiting for transfers between devices: 213 us -> 97.5 us
  local copies, waits for them, and re-layouts: 108 us -> 1.22 us
  starting transfers between devices: 38 us -> 64.5 us
    all_to_all x4 -> x1, waiting for transfers between devices: 213 us -> 0.01 us  [shards(): blocks = lax.all_to_all(flat.reshape(32, 32, rows), PLANE, 0, 0, tiled=True)]
    another operation x30 -> x2, other arithmetic: 172 us -> 0.09 us  [the longest x1 0.08 us: shards(): at = jnp.stack([at_y, at_c, (at_x * 8 + at_z) * out_rows]).astype(jnp.int32)]
    dot_general x4 -> x0, matrix products: 131 us -> none  [the longest x1 83.9 us: shards(): before = jnp.dot(sylvester(row_dev), signed, precision=exact_mode)]
    pallas_call x0 -> x5, Pallas kernels: none -> 119 us  [the longest x1 74.2 us: factored(): pl.pallas_call(factor_kernel, in_specs=[pl.BlockSpec(memory_space=pltpu.S...]
    ppermute x0 -> x26, waiting for transfers between devices: none -> 97.5 us  [from_ahead(): lax.ppermute(array, axis, [((i + shift) % size, i) for i in range(size)])]
    ppermute x0 -> x26, starting transfers between devices: none -> 55.7 us  [from_ahead(): lax.ppermute(array, axis, [((i + shift) % size, i) for i in range(size)])]
    all_to_all x4 -> x1, starting transfers between devices: 38 us -> 8.77 us  [shards(): blocks = lax.all_to_all(flat.reshape(32, 32, rows), PLANE, 0, 0, tiled=True)]
    dot_general x3 -> x0, local copies, waits for them, and re-layouts: 27.3 us -> none  [the longest x2 18.3 us: shards(): jnp.einsum('kn,km->nm', flat_rows * weights[:, None], flat_rows, precisio...]
  transfers between devices with their start and end apart: 4 -> 27, of which waited for: 3 -> 11; matrix products, arithmetic and copies ran while one was open for 12% -> 0% of each run, Pallas kernels for 0% -> 4%
where the time goes in v1:
time: 348 us; the launch traced here: 347 us
  Pallas kernels  119 us (34%)
  waiting for transfers between devices  97.5 us (28%)
  blocking collectives  64.8 us (19%)
  starting transfers between devices  64.5 us (19%)
    ppermute x26, waiting for transfers between devices, from_ahead(): lax.ppermute(array, axis, [((i + shift) % size, i) for i in range(size)])  97.5 us
    pallas_call x1, Pallas kernels, factored(): pl.pallas_call(factor_kernel, in_specs=[pl.BlockSpec(memory_space=pltpu.S...  74.2 us
    ppermute x26, starting transfers between devices, from_ahead(): lax.ppermute(array, axis, [((i + shift) % size, i) for i in range(size)])  55.7 us
    all_to_all x1, blocking collectives, shards(): arrived = lax.all_to_all(ours, ('z', 'x'), 0, 0, tiled=True)  28.4 us
    pallas_call x1, Pallas kernels, picked(): pl.pallas_call(pick_kernel, grid=(8,), in_specs=[pl.BlockSpec((32, 32, 25...  21.5 us
    all_to_all x1, blocking collectives, shards(): share = lax.all_to_all(tiles, ('z', 'x'), 0, 0, tiled=True).sum(axis=0)  18.7 us
    all_to_all x1, blocking collectives, shards(): lax.all_to_all(whole, ('z', 'x'), 0, 0, tiled=True).reshape(6, TILE, TILE)  17.6 us
    pallas_call x1, Pallas kernels, sampled_signs(): pl.pallas_call(signs_kernel, grid=(32,), in_specs=[pl.BlockSpec(memory_sp...  12.3 us
  transfers between devices with their start and end apart: 27, of which 11 were waited for; matrix products, arithmetic and copies ran while one was open for 0% of the time, Pallas kernels for 4%

profile of v1, /device:TPU:1, one launch (start us, length us, event | category | flops | bytes accessed | tf_op | source)
XLA Modules:
  0.0 347.0 jit_solution(6839361376583222482)
XLA Ops:
  0.7 9.9 %turn.1 = f32[1024,2048]{1,0:T(8,128)} custom-call(s32[16,128]{1,0:T(8,128)S(1)} %bitcast.70, f32[2048,1024]{1,0:T(8,128)} %in_ref.1), custom_call_target="tpu_custom_call" | custom-call | tf_op jit(solution)/shard_map/turn/pallas_call | solution.py:35
  10.6 8.8 %all-to-all-start = ((f32[32,32,2048]{2,1,0:T(8,128)}), f32[32,32,2048]{2,1,0:T(8,128)}, u32[]{:S(2)}, u32[]{:S(2)}) async-start(f32[32,32,2048]{2,1,0:T(8,128)} %bitcast.71), calls=%async_computation | async-start | bytes 16777216 | tf_op jit(solution)/shard_map/all_to_all | solution.py:317
  19.8 1.0 collective-permute-done
  20.9 2.9 collective-permute-start.1
  24.8 59.0 %collective-permute-done.1 = s32[2,32]{1,0:T(2,128)S(1)} collective-permute-done((s32[2,32]{1,0:T(2,128)S(1)}, s32[2,32]{1,0:T(2,128)S(1)}, u32[]{:S(2)}, u32[]{:S(2)}) %collective-permute-start.1) | collective-permute-done | bytes 288 | tf_op jit(solution)/shard_map/ppermute | solution.py:295
  83.8 26.9 %collective-permute-done.2 = s32[2,32]{1,0:T(2,128)S(1)} collective-permute-done((s32[2,32]{1,0:T(2,128)S(1)}, s32[2,32]{1,0:T(2,128)S(1)}, u32[]{:S(2)}, u32[]{:S(2)}) %collective-permute-start.2) | collective-permute-done | bytes 288 | tf_op jit(solution)/shard_map/ppermute | solution.py:295
  110.8 3.7 %collective-permute-start.4 = (s32[4,2,32]{2,1,0:T(2,128)S(1)}, s32[4,2,32]{2,1,0:T(2,128)S(1)}, u32[]{:S(2)}, u32[]{:S(2)}) collective-permute-start(s32[4,2,32]{2,1,0:T(2,128)S(1)} %get-tuple-element.12), channel_id=1, source_target_pairs={{64,0},{128,64},{192,128},{0,192},{65,1},{129,65},{193,129},{1,193... | collective-permute-start | bytes 3080 | tf_op jit(solution)/shard_map/ppermute | solution.py:295
  115.2 2.6 collective-permute-done.4
  117.8 1.7 collective-permute-done.5
  119.6 5.7 %collective-permute-start.7 = (s32[4,4,2,32]{3,2,1,0:T(2,128)S(1)}, s32[4,4,2,32]{3,2,1,0:T(2,128)S(1)}, u32[]{:S(2)}, u32[]{:S(2)}) collective-permute-start(s32[4,4,2,32]{3,2,1,0:T(2,128)S(1)} %get-tuple-element.10), channel_id=1, source_target_pairs={{8,0},{16,8},{24,16},{32,24},{40,32},{48,40},{56,48},{0,56},{9,1},... | collective-permute-start | bytes 12296 | tf_op jit(solution)/shard_map/ppermute | solution.py:295
  125.3 1.2 collective-permute-start.8
  126.9 4.5 %collective-permute-start.10 = (s32[4,4,2,32]{3,2,1,0:T(2,128)S(1)}, s32[4,4,2,32]{3,2,1,0:T(2,128)S(1)}, u32[]{:S(2)}, u32[]{:S(2)}) collective-permute-start(s32[4,4,2,32]{3,2,1,0:T(2,128)S(1)} %get-tuple-element.10), channel_id=1, source_target_pairs={{32,0},{40,8},{48,16},{56,24},{0,32},{8,40},{16,48},{24,56},{33,1}... | collective-permute-start | bytes 12296 | tf_op jit(solution)/shard_map/ppermute | solution.py:295
  131.4 2.2 collective-permute-start.12
  133.6 1.4 collective-permute-start.13
  135.0 2.0 collective-permute-done.11
  137.7 12.3 %signs.1 = (bf16[32,256,256]{2,1,0:T(8,128)(2,1)}, f32[32,8,256]{2,1,0:T(8,128)S(1)}) custom-call(s32[1]{0:T(128)} %bitcast.5.z_ref, s32[32,256]{1,0:T(8,128)S(1)} %reshape.25.sample_ref), custom_call_target="tpu_custom_call" | custom-call | tf_op jit(solution)/shard_map/signs/pallas_call | solution.py:69
  150.0 21.5 %pick.1 = f32[32,32,256]{2,1,0:T(8,128)S(1)} custom-call(f32[32,32,2048]{2,1,0:T(8,128)} %all-to-all-done.in_ref, bf16[32,256,256]{2,1,0:T(8,128)(2,1)} %get-tuple-element.7.low_ref, f32[32,8,256]{2,1,0:T(8,128)S(1)} %get-tuple-element.8.high_ref), custom_call_target="tpu_custom_call" | custom-call | tf_op jit(solution)/shard_map/pick/pallas_call | solution.py:131
  171.5 28.4 %all_to_all.20 = f32[32,32,256]{2,1,0:T(8,128)S(1)} all-to-all(f32[32,32,256]{2,1,0:T(8,128)S(1)} %pick.1), channel_id=1, replica_groups=mesh['x'=4,'z'=8,'y'=4,'c'=2] {'z','x'}, dimensions={0} | all-to-all | bytes 2097152 | tf_op jit(solution)/shard_map/all_to_all | solution.py:320
  200.0 2.8 collective-permute-start.14
  202.8 2.3 collective-permute-start.15
  205.1 5.8 %collective-permute-start.16 = (f32[128,256]{1,0:T(8,128)S(1)}, f32[128,256]{1,0:T(8,128)S(1)}, u32[]{:S(2)}, u32[]{:S(2)}) collective-permute-start(f32[128,256]{1,0:T(8,128)S(1)} %bitcast_reduce_fusion.own_ref), channel_id=1, source_target_pairs={{1,0},{0,1},{3,2},{2,3},{5,4},{4,5},{7,6},{6,7},{9,8},{8,9},{11,10... | collective-permute-start | bytes 393224 | tf_op jit(solution)/shard_map/ppermute | solution.py:295
  210.9 1.1 collective-permute-start.17
  212.0 3.1 collective-permute-start.18
  215.0 1.0 collective-permute-done.18.o_far_ref
  216.8 18.7 %all_to_all.21 = f32[32,24,128]{2,1,0:T(8,128)S(1)} all-to-all(f32[32,24,128]{2,1,0:T(8,128)S(1)} %bitcast.69), channel_id=1, replica_groups=mesh['x'=4,'z'=8,'y'=4,'c'=2] {'z','x'}, dimensions={0} | all-to-all | bytes 786432 | tf_op jit(solution)/shard_map/all_to_all | solution.py:325
  235.6 17.6 %all_to_all.22 = f32[32,24,128]{2,1,0:T(8,128)S(1)} all-to-all(f32[32,24,128]{2,1,0:T(8,128)S(1)} %broadcast_in_dim.2), channel_id=1, replica_groups=mesh['x'=4,'z'=8,'y'=4,'c'=2] {'z','x'}, dimensions={0} | all-to-all | bytes 786432 | tf_op jit(solution)/shard_map/all_to_all | solution.py:327
  253.2 2.5 collective-permute-start.19
  256.4 4.2 %collective-permute-start.22 = (f32[6,128,128]{2,1,0:T(8,128)S(1)}, f32[6,128,128]{2,1,0:T(8,128)S(1)}, u32[]{:S(2)}, u32[]{:S(2)}) collective-permute-start(f32[6,128,128]{2,1,0:T(8,128)S(1)} %bitcast.67), channel_id=1, source_target_pairs={{1,0},{0,1},{3,2},{2,3},{5,4},{4,5},{7,6},{6,7},{9,8},{8,9},{11,10... | collective-permute-start | bytes 1179656 | tf_op jit(solution)/shard_map/ppermute | solution.py:295
  260.6 1.8 collective-permute-done.19.refs_1_
  262.4 8.3 %collective-permute-start.23 = (f32[6,128,128]{2,1,0:T(8,128)S(1)}, f32[6,128,128]{2,1,0:T(8,128)S(1)}, u32[]{:S(2)}, u32[]{:S(2)}) collective-permute-start(f32[6,128,128]{2,1,0:T(8,128)S(1)} %collective-permute-done.19.refs_1_), channel_id=1, source_target_pairs={{1,0},{0,1},{3,2},{2,3},{5,4},{4,5},{7,6},{6,7},{9,8},{8,9},{11,10... | collective-permute-start | bytes 1179656 | tf_op jit(solution)/shard_map/ppermute | solution.py:295
  270.7 1.0 collective-permute-start.25
  272.9 74.2 %factor.1 = f32[32,1024]{1,0:T(8,128)} custom-call(s32[3]{0:T(128)S(1)} %pad_add_fusion.1.at_ref, f32[6,128,128]{2,1,0:T(8,128)S(1)} %bitcast.68, f32[6,128,128]{2,1,0:T(8,128)S(1)} %collective-permute-done.19.refs_1_, f32[4,128,128]{2,1,0:T(8,128)S(1)} %collective-permute-done.20.refs_2_, f32[4,128,128]{2,1,0:T(8,128)S(1)} %collective-permute-done.21.refs_3_, ...), custom_call_target="tpu_custom_call" | custom-call | tf_op jit(solution)/shard_map/factor/pallas_call | solution.py:278
  (75 shorter events, 7.0 us)
Async XLA Ops:
  0.0 0.7 copy-start
  10.6 8.8 %copy-start.1 = (s32[32]{0:T(128)S(1)}, s32[32]{0:T(128)}, u32[]{:S(2)}) copy-start(s32[32]{0:T(128)} %param.5) | copy-start | bytes 388
  10.6 139.4 %all-to-all-start = ((f32[32,32,2048]{2,1,0:T(8,128)}), f32[32,32,2048]{2,1,0:T(8,128)}, u32[]{:S(2)}, u32[]{:S(2)}) async-start(f32[32,32,2048]{2,1,0:T(8,128)} %bitcast.71), calls=%async_computation | async-start | bytes 16777216 | tf_op jit(solution)/shard_map/all_to_all | solution.py:317
  19.4 1.4 collective-permute-start
  20.9 63.0 %collective-permute-start.1 = (s32[2,32]{1,0:T(2,128)S(1)}, s32[2,32]{1,0:T(2,128)S(1)}, u32[]{:S(2)}, u32[]{:S(2)}) collective-permute-start(s32[2,32]{1,0:T(2,128)S(1)} %get-tuple-element.14), channel_id=1, source_target_pairs={{2,0},{4,2},{6,4},{0,6},{3,1},{5,3},{7,5},{1,7},{10,8},{12,10},{14... | collective-permute-start | bytes 776 | tf_op jit(solution)/shard_map/ppermute | solution.py:295
  23.7 87.0 %collective-permute-start.2 = (s32[2,32]{1,0:T(2,128)S(1)}, s32[2,32]{1,0:T(2,128)S(1)}, u32[]{:S(2)}, u32[]{:S(2)}) collective-permute-start(s32[2,32]{1,0:T(2,128)S(1)} %get-tuple-element.14), channel_id=1, source_target_pairs={{4,0},{6,2},{0,4},{2,6},{5,1},{7,3},{1,5},{3,7},{12,8},{14,10},{8,... | collective-permute-start | bytes 776 | tf_op jit(solution)/shard_map/ppermute | solution.py:295
  24.3 86.5 %collective-permute-start.3 = (s32[2,32]{1,0:T(2,128)S(1)}, s32[2,32]{1,0:T(2,128)S(1)}, u32[]{:S(2)}, u32[]{:S(2)}) collective-permute-start(s32[2,32]{1,0:T(2,128)S(1)} %get-tuple-element.14), channel_id=1, source_target_pairs={{6,0},{0,2},{2,4},{4,6},{7,1},{1,3},{3,5},{5,7},{14,8},{8,10},{10,... | collective-permute-start | bytes 776 | tf_op jit(solution)/shard_map/ppermute | solution.py:295
  110.8 7.0 %collective-permute-start.4 = (s32[4,2,32]{2,1,0:T(2,128)S(1)}, s32[4,2,32]{2,1,0:T(2,128)S(1)}, u32[]{:S(2)}, u32[]{:S(2)}) collective-permute-start(s32[4,2,32]{2,1,0:T(2,128)S(1)} %get-tuple-element.12), channel_id=1, source_target_pairs={{64,0},{128,64},{192,128},{0,192},{65,1},{129,65},{193,129},{1,193... | collective-permute-start | bytes 3080 | tf_op jit(solution)/shard_map/ppermute | solution.py:295
  114.5 5.0 %collective-permute-start.5 = (s32[4,2,32]{2,1,0:T(2,128)S(1)}, s32[4,2,32]{2,1,0:T(2,128)S(1)}, u32[]{:S(2)}, u32[]{:S(2)}) collective-permute-start(s32[4,2,32]{2,1,0:T(2,128)S(1)} %get-tuple-element.12), channel_id=1, source_target_pairs={{128,0},{192,64},{0,128},{64,192},{129,1},{193,65},{1,129},{65,193... | collective-permute-start | bytes 3080 | tf_op jit(solution)/shard_map/ppermute | solution.py:295
  114.5 5.0 %collective-permute-start.6 = (s32[4,2,32]{2,1,0:T(2,128)S(1)}, s32[4,2,32]{2,1,0:T(2,128)S(1)}, u32[]{:S(2)}, u32[]{:S(2)}) collective-permute-start(s32[4,2,32]{2,1,0:T(2,128)S(1)} %get-tuple-element.12), channel_id=1, source_target_pairs={{192,0},{0,64},{64,128},{128,192},{193,1},{1,65},{65,129},{129,193... | collective-permute-start | bytes 3080 | tf_op jit(solution)/shard_map/ppermute | solution.py:295
  119.6 11.8 %collective-permute-start.7 = (s32[4,4,2,32]{3,2,1,0:T(2,128)S(1)}, s32[4,4,2,32]{3,2,1,0:T(2,128)S(1)}, u32[]{:S(2)}, u32[]{:S(2)}) collective-permute-start(s32[4,4,2,32]{3,2,1,0:T(2,128)S(1)} %get-tuple-element.10), channel_id=1, source_target_pairs={{8,0},{16,8},{24,16},{32,24},{40,32},{48,40},{56,48},{0,56},{9,1},... | collective-permute-start | bytes 12296 | tf_op jit(solution)/shard_map/ppermute | solution.py:295
  125.3 8.3 %collective-permute-start.8 = (s32[4,4,2,32]{3,2,1,0:T(2,128)S(1)}, s32[4,4,2,32]{3,2,1,0:T(2,128)S(1)}, u32[]{:S(2)}, u32[]{:S(2)}) collective-permute-start(s32[4,4,2,32]{3,2,1,0:T(2,128)S(1)} %get-tuple-element.10), channel_id=1, source_target_pairs={{16,0},{24,8},{32,16},{40,24},{48,32},{56,40},{0,48},{8,56},{17,1}... | collective-permute-start | bytes 12296 | tf_op jit(solution)/shard_map/ppermute | solution.py:295
  126.5 8.5 %collective-permute-start.9 = (s32[4,4,2,32]{3,2,1,0:T(2,128)S(1)}, s32[4,4,2,32]{3,2,1,0:T(2,128)S(1)}, u32[]{:S(2)}, u32[]{:S(2)}) collective-permute-start(s32[4,4,2,32]{3,2,1,0:T(2,128)S(1)} %get-tuple-element.10), channel_id=1, source_target_pairs={{24,0},{32,8},{40,16},{48,24},{56,32},{0,40},{8,48},{16,56},{25,1}... | collective-permute-start | bytes 12296 | tf_op jit(solution)/shard_map/ppermute | solution.py:295
  126.9 8.1 %collective-permute-start.10 = (s32[4,4,2,32]{3,2,1,0:T(2,128)S(1)}, s32[4,4,2,32]{3,2,1,0:T(2,128)S(1)}, u32[]{:S(2)}, u32[]{:S(2)}) collective-permute-start(s32[4,4,2,32]{3,2,1,0:T(2,128)S(1)} %get-tuple-element.10), channel_id=1, source_target_pairs={{32,0},{40,8},{48,16},{56,24},{0,32},{8,40},{16,48},{24,56},{33,1}... | collective-permute-start | bytes 12296 | tf_op jit(solution)/shard_map/ppermute | solution.py:295
  131.4 5.6 %collective-permute-start.11 = (s32[4,4,2,32]{3,2,1,0:T(2,128)S(1)}, s32[4,4,2,32]{3,2,1,0:T(2,128)S(1)}, u32[]{:S(2)}, u32[]{:S(2)}) collective-permute-start(s32[4,4,2,32]{3,2,1,0:T(2,128)S(1)} %get-tuple-element.10), channel_id=1, source_target_pairs={{40,0},{48,8},{56,16},{0,24},{8,32},{16,40},{24,48},{32,56},{41,1}... | collective-permute-start | bytes 12296 | tf_op jit(solution)/shard_map/ppermute | solution.py:295
  131.4 5.6 %collective-permute-start.12 = (s32[4,4,2,32]{3,2,1,0:T(2,128)S(1)}, s32[4,4,2,32]{3,2,1,0:T(2,128)S(1)}, u32[]{:S(2)}, u32[]{:S(2)}) collective-permute-start(s32[4,4,2,32]{3,2,1,0:T(2,128)S(1)} %get-tuple-element.10), channel_id=1, source_target_pairs={{48,0},{56,8},{0,16},{8,24},{16,32},{24,40},{32,48},{40,56},{49,1}... | collective-permute-start | bytes 12296 | tf_op jit(solution)/shard_map/ppermute | solution.py:295
  133.6 3.8 %collective-permute-start.13 = (s32[4,4,2,32]{3,2,1,0:T(2,128)S(1)}, s32[4,4,2,32]{3,2,1,0:T(2,128)S(1)}, u32[]{:S(2)}, u32[]{:S(2)}) collective-permute-start(s32[4,4,2,32]{3,2,1,0:T(2,128)S(1)} %get-tuple-element.10), channel_id=1, source_target_pairs={{56,0},{0,8},{8,16},{16,24},{24,32},{32,40},{40,48},{48,56},{57,1}... | collective-permute-start | bytes 12296 | tf_op jit(solution)/shard_map/ppermute | solution.py:295
  200.0 10.9 %collective-permute-start.14 = (f32[128,256]{1,0:T(8,128)S(1)}, f32[128,256]{1,0:T(8,128)S(1)}, u32[]{:S(2)}, u32[]{:S(2)}) collective-permute-start(f32[128,256]{1,0:T(8,128)S(1)} %bitcast_reduce_fusion.own_ref), channel_id=1, source_target_pairs={{2,0},{4,2},{6,4},{0,6},{3,1},{5,3},{7,5},{1,7},{10,8},{12,10},{14... | collective-permute-start | bytes 393224 | tf_op jit(solution)/shard_map/ppermute | solution.py:295
  202.8 9.2 %collective-permute-start.15 = (f32[128,256]{1,0:T(8,128)S(1)}, f32[128,256]{1,0:T(8,128)S(1)}, u32[]{:S(2)}, u32[]{:S(2)}) collective-permute-start(f32[128,256]{1,0:T(8,128)S(1)} %bitcast_reduce_fusion.own_ref), channel_id=1, source_target_pairs={{4,0},{6,2},{0,4},{2,6},{5,1},{7,3},{1,5},{3,7},{12,8},{14,10},{8,... | collective-permute-start | bytes 393224 | tf_op jit(solution)/shard_map/ppermute | solution.py:295
  205.1 9.9 %collective-permute-start.16 = (f32[128,256]{1,0:T(8,128)S(1)}, f32[128,256]{1,0:T(8,128)S(1)}, u32[]{:S(2)}, u32[]{:S(2)}) collective-permute-start(f32[128,256]{1,0:T(8,128)S(1)} %bitcast_reduce_fusion.own_ref), channel_id=1, source_target_pairs={{1,0},{0,1},{3,2},{2,3},{5,4},{4,5},{7,6},{6,7},{9,8},{8,9},{11,10... | collective-permute-start | bytes 393224 | tf_op jit(solution)/shard_map/ppermute | solution.py:295
  210.9 4.1 %collective-permute-start.17 = (f32[128,256]{1,0:T(8,128)S(1)}, f32[128,256]{1,0:T(8,128)S(1)}, u32[]{:S(2)}, u32[]{:S(2)}) collective-permute-start(f32[128,256]{1,0:T(8,128)S(1)} %collective-permute-done.14.near_ref), channel_id=1, source_target_pairs={{1,0},{0,1},{3,2},{2,3},{5,4},{4,5},{7,6},{6,7},{9,8},{8,9},{11,10... | collective-permute-start | bytes 393224 | tf_op jit(solution)/shard_map/ppermute | solution.py:295
  212.0 4.1 %collective-permute-start.18 = (f32[128,256]{1,0:T(8,128)S(1)}, f32[128,256]{1,0:T(8,128)S(1)}, u32[]{:S(2)}, u32[]{:S(2)}) collective-permute-start(f32[128,256]{1,0:T(8,128)S(1)} %collective-permute-done.15.far_ref), channel_id=1, source_target_pairs={{1,0},{0,1},{3,2},{2,3},{5,4},{4,5},{7,6},{6,7},{9,8},{8,9},{11,10... | collective-permute-start | bytes 393224 | tf_op jit(solution)/shard_map/ppermute | solution.py:295
  253.2 9.2 %collective-permute-start.19 = (f32[6,128,128]{2,1,0:T(8,128)S(1)}, f32[6,128,128]{2,1,0:T(8,128)S(1)}, u32[]{:S(2)}, u32[]{:S(2)}) collective-permute-start(f32[6,128,128]{2,1,0:T(8,128)S(1)} %bitcast.65), channel_id=1, source_target_pairs={{2,0},{4,2},{6,4},{0,6},{3,1},{5,3},{7,5},{1,7},{10,8},{12,10},{14... | collective-permute-start | bytes 1179656 | tf_op jit(solution)/shard_map/ppermute | solution.py:295
  255.8 15.0 %collective-permute-start.20 = (f32[4,128,128]{2,1,0:T(8,128)S(1)}, f32[4,128,128]{2,1,0:T(8,128)S(1)}, u32[]{:S(2)}, u32[]{:S(2)}) collective-permute-start(f32[4,128,128]{2,1,0:T(8,128)S(1)} %slice.5), channel_id=1, source_target_pairs={{4,0},{6,2},{0,4},{2,6},{5,1},{7,3},{1,5},{3,7},{12,8},{14,10},{8,... | collective-permute-start | bytes 786440 | tf_op jit(solution)/shard_map/ppermute | solution.py:295
  256.4 14.4 %collective-permute-start.21 = (f32[4,128,128]{2,1,0:T(8,128)S(1)}, f32[4,128,128]{2,1,0:T(8,128)S(1)}, u32[]{:S(2)}, u32[]{:S(2)}) collective-permute-start(f32[4,128,128]{2,1,0:T(8,128)S(1)} %slice.5), channel_id=1, source_target_pairs={{6,0},{0,2},{2,4},{4,6},{7,1},{1,3},{3,5},{5,7},{14,8},{8,10},{10,... | collective-permute-start | bytes 786440 | tf_op jit(solution)/shard_map/ppermute | solution.py:295
  256.4 15.3 %collective-permute-start.22 = (f32[6,128,128]{2,1,0:T(8,128)S(1)}, f32[6,128,128]{2,1,0:T(8,128)S(1)}, u32[]{:S(2)}, u32[]{:S(2)}) collective-permute-start(f32[6,128,128]{2,1,0:T(8,128)S(1)} %bitcast.67), channel_id=1, source_target_pairs={{1,0},{0,1},{3,2},{2,3},{5,4},{4,5},{7,6},{6,7},{9,8},{8,9},{11,10... | collective-permute-start | bytes 1179656 | tf_op jit(solution)/shard_map/ppermute | solution.py:295
  262.4 10.5 %collective-permute-start.23 = (f32[6,128,128]{2,1,0:T(8,128)S(1)}, f32[6,128,128]{2,1,0:T(8,128)S(1)}, u32[]{:S(2)}, u32[]{:S(2)}) collective-permute-start(f32[6,128,128]{2,1,0:T(8,128)S(1)} %collective-permute-done.19.refs_1_), channel_id=1, source_target_pairs={{1,0},{0,1},{3,2},{2,3},{5,4},{4,5},{7,6},{6,7},{9,8},{8,9},{11,10... | collective-permute-start | bytes 1179656 | tf_op jit(solution)/shard_map/ppermute | solution.py:295
  270.7 1.7 collective-permute-start.24
  270.7 2.1 collective-permute-start.25

commit v2 on v1

--- a/solution.py
+++ b/solution.py
@@ -16,22 +16,32 @@
 COLS = 1024
 BLOCKS = 256
 TILE = 128
+SHARE = 32
+CHUNKS = (32,)
+STEPS = 4
 
 
 def vmem(limit=100):
     return pltpu.CompilerParams(vmem_limit_bytes=limit * 1024 * 1024 // 2)
 
 
-def turn_kernel(sign_ref, in_ref, out_ref):
+def turn_kernel(sign_ref, in_ref, *out_refs):
     for t in range(in_ref.shape[0] // TILE):
         rows = slice(t * TILE, (t + 1) * TILE)
-        sign = sign_ref[t : t + 1, :].astype(F32)
-        out_ref[:, rows] = in_ref[rows, :].T * sign
+        lines = in_ref[rows, :].T * sign_ref[t : t + 1, :].astype(F32)
+        for group in range(TILE // SHARE):
+            first = group * SHARE
+            for out_ref in out_refs:
+                count = out_ref.shape[0] * SHARE // TILE
+                into = slice(group * count, (group + 1) * count)
+                out_ref[into, rows] = lines[first : first + count, :]
+                first += count
 
 
 def turned(matrix, row_signs):
     rows, cols = matrix.shape
     signs = row_signs.reshape(rows // TILE, TILE)
+    groups = TILE // SHARE
     return pl.pallas_call(
         turn_kernel,
         grid=(cols // TILE,),
@@ -39,8 +49,8 @@
             pl.BlockSpec(signs.shape, lambda i: (0, 0)),
             pl.BlockSpec((rows, TILE), lambda i: (0, i)),
         ],
-        out_specs=pl.BlockSpec((TILE, rows), lambda i: (i, 0)),
-        out_shape=jax.ShapeDtypeStruct((cols, rows), F32),
+        out_specs=[pl.BlockSpec((groups * n, rows), lambda i: (i, 0)) for n in CHUNKS],
+        out_shape=[jax.ShapeDtypeStruct((cols * n // SHARE, rows), F32) for n in CHUNKS],
         compiler_params=vmem(),
         name="turn",
     )(signs, matrix)
@@ -100,45 +110,58 @@
 
 
 def pick_kernel(in_ref, low_ref, high_ref, out_ref, parts_ref):
-    wh = pl.program_id(0)
-
-    @pl.when(wh == 0)
+    step = pl.program_id(0)
+    count = in_ref.shape[1]
+
+    @pl.when(step < STEPS)
     def _():
-        out_ref[...] = jnp.zeros_like(out_ref)
-
-    for row in range(0, 32, 16):
-        for lane in range(0, 256, TILE):
-            lanes = slice(lane, lane + TILE)
-            values = butterflies([in_ref[p, row : row + 16, lanes] for p in range(32)])
-            for p in range(32):
-                rest = values[p]
-                for part in range(3):
-                    piece = rest.astype(BF16)
-                    parts_ref[p, 32 * part + row : 32 * part + row + 16, lanes] = piece
-                    if part < 2:
-                        rest = rest - piece.astype(F32)
-
-    def one(p, carry):
-        got = jnp.dot(parts_ref[p], low_ref[p], preferred_element_type=F32)
-        got = got[0:32] + got[32:64] + got[64:96]
-        out_ref[p] = out_ref[p] + got * high_ref[p, pl.ds(wh, 1), :]
-        return carry
-
-    lax.fori_loop(0, 32, one, 0, unroll=4)
+        for half in range(in_ref.shape[2] // 256):
+            wh = step * (in_ref.shape[2] // 256) + half
+            for row in range(0, count, 16):
+                for lane in range(0, 256, TILE):
+                    lanes = slice(lane, lane + TILE)
+                    at = slice(half * 256 + lane, half * 256 + lane + TILE)
+                    values = butterflies([in_ref[p, row : row + 16, at] for p in range(32)])
+                    for p in range(32):
+                        rest = values[p]
+                        for part in range(3):
+                            piece = rest.astype(BF16)
+                            first = count * part + row
+                            parts_ref[p, wh, first : first + 16, lanes] = piece
+                            if part < 2:
+                                rest = rest - piece.astype(F32)
+
+    @pl.when(step >= STEPS)
+    def _():
+        for n in range(out_ref.shape[0]):
+            p = (step - STEPS) * out_ref.shape[0] + n
+            lines = parts_ref[p].reshape(24 * count, 256)
+            got = jnp.dot(lines, low_ref[n], preferred_element_type=F32)
+            total = jnp.zeros((count, 256), F32)
+            for wh in range(8):
+                some = got[3 * count * wh : 3 * count * (wh + 1)]
+                some = some[0:count] + some[count : 2 * count] + some[2 * count :]
+                total = total + some * high_ref[n, wh : wh + 1, :]
+            out_ref[n] = total
 
 
 def picked(blocks, low, high):
+    count, rows = blocks.shape[1:]
+    group = 32 // STEPS
+    late = lambda i: (jnp.maximum(i - STEPS, 0), 0, 0)
     return pl.pallas_call(
         pick_kernel,
-        grid=(8,),
+        grid=(2 * STEPS,),
         in_specs=[
-            pl.BlockSpec((32, 32, 256), lambda i: (0, 0, i)),
-            pl.BlockSpec((32, 256, 256), lambda i: (0, 0, 0)),
-            pl.BlockSpec((32, 8, 256), lambda i: (0, 0, 0)),
-        ],
-        out_specs=pl.BlockSpec((32, 32, 256), lambda i: (0, 0, 0)),
-        out_shape=jax.ShapeDtypeStruct((32, 32, 256), F32),
-        scratch_shapes=[pltpu.VMEM((32, 96, 256), BF16)],
+            pl.BlockSpec(
+                (32, count, rows // STEPS), lambda i: (0, 0, jnp.minimum(i, STEPS - 1))
+            ),
+            pl.BlockSpec((group, 256, 256), late),
+            pl.BlockSpec((group, 8, 256), late),
+        ],
+        out_specs=pl.BlockSpec((group, count, 256), late),
+        out_shape=jax.ShapeDtypeStruct((32, count, 256), F32),
+        scratch_shapes=[pltpu.VMEM((32, 8, 3 * count, 256), BF16)],
         compiler_params=vmem(),
         name="pick",
     )(blocks, low, high)
@@ -180,7 +203,7 @@
 
 def factor_kernel(at_ref, *refs):
     tile_refs = refs[:8]
-    out_ref, work, left = refs[8:]
+    out_ref, work, left, heads, scales = refs[8:]
     y, c, row0 = at_ref[0], at_ref[1], at_ref[2]
     for n, ref in enumerate(tile_refs):
         shift, other = n % 4, n // 4
@@ -206,63 +229,77 @@
         def rows(i):
             return pl.ds(pl.multiple_of(base + 8 * i, 8), 8)
 
+        for above in range(1, 8):
+
+            @pl.when(j == above)
+            def _(above=above):
+                deep = above * TILE
+                mine = work[above, 0:deep, :].T
+                for k in range(above, 8):
+                    into = slice(deep, deep + TILE)
+                    work[k, into, :] = work[k, into, :] - jnp.dot(
+                        mine,
+                        work[k, 0:deep, :],
+                        precision=EXACT,
+                        preferred_element_type=F32,
+                    )
+
+        tile = [work[j, rows(i), :] for i in range(16)]
+        columns = [over_lanes(tile[0], m) for m in range(8)]
         for t in range(16):
-            head = work[j, rows(t), :]
-            columns = [over_lanes(head, 8 * t + m) for m in range(8)]
-            roots, lefts, pairs = [], [], {}
+            head = tile[t]
+            nexts = []
+            if t < 15:
+                nexts = [over_lanes(tile[t + 1], 8 * (t + 1) + q) for q in range(8)]
+            inverses, pairs = [], {}
             scale = jnp.zeros((8, TILE), F32)
             for m in range(8):
-                root = inverse_root(over_rows(columns[m], m))
-                column = columns[m] * root
+                pivot = over_rows(columns[m], m)
+                inverse = 1.0 / pivot
                 for q in range(m + 1, 8):
-                    pairs[q, m] = over_rows(column, q)
-                    columns[q] = columns[q] - column * pairs[q, m]
-                roots.append(root)
-                lefts.append(jnp.where(row_of > m, column, 0.0))
-                scale = jnp.where(row_of == m, root, scale)
+                    entry = over_rows(columns[m], q)
+                    columns[q] = columns[q] - (columns[m] * entry) * inverse
+                    pairs[q, m] = entry * inverse
+                masked = jnp.where(row_of > m, columns[m] * inverse, 0.0)
+                heads[t, m] = masked
+                head = head - masked * over_rows(head, m)
+                inverses.append(inverse)
+                scale = jnp.where(row_of == m, inverse_root(pivot), scale)
+            scales[t] = scale
+            work[j, rows(t), :] = head * scale
+            lines = [over_rows(head, m) for m in range(8)]
             for i in range(t + 1, 16):
-                block = work[j, rows(i), :]
-                got = []
+                got, scaled = [], []
                 for m in range(8):
-                    value = over_lanes(block, 8 * t + m)
+                    value = over_lanes(tile[i], 8 * t + m)
                     for q in range(m):
                         value = value - got[q] * pairs[m, q]
-                    got.append(value * roots[m])
-                    left[i, m] = got[m]
-
-            def one_tile(k, carry, t=t, lefts=lefts, roots=roots, scale=scale):
-                head = work[k, rows(t), :]
+                    got.append(value)
+                    scaled.append(value * inverses[m])
+                    left[t, i, m] = scaled[m]
                 for m in range(8):
-                    head = head - lefts[m] * (over_rows(head, m) * roots[m])
-                head = head * scale
-                work[k, rows(t), :] = head
+                    tile[i] = tile[i] - scaled[m] * lines[m]
+                if i == t + 1:
+                    for q in range(8):
+                        for m in range(8):
+                            nexts[q] = nexts[q] - scaled[m] * over_rows(got[m], q)
+            columns = nexts
+
+        def one_tile(k, carry):
+            lower = [work[k, rows(i), :] for i in range(16)]
+            for t in range(16):
+                head = lower[t]
+                for m in range(8):
+                    head = head - heads[t, m] * over_rows(head, m)
+                work[k, rows(t), :] = head * scales[t]
                 if t < 15:
                     lines = [over_rows(head, m) for m in range(8)]
                     for i in range(t + 1, 16):
-                        block = work[k, rows(i), :]
                         for m in range(8):
-                            block = block - left[i, m] * lines[m]
-                        work[k, rows(i), :] = block
-                return carry
-
-            lax.fori_loop(j, 8, one_tile, 0)
-
-        for done in range(7):
-
-            @pl.when(j == done)
-            def _(done=done):
-                rows_done = slice(done * TILE, (done + 1) * TILE)
-                for i in range(done + 1, 8):
-                    turned_tile = work[i, rows_done, :].T
-                    for k in range(i, 8):
-                        into = slice(i * TILE, (i + 1) * TILE)
-                        work[k, into, :] = work[k, into, :] - jnp.dot(
-                            turned_tile,
-                            work[k, rows_done, :],
-                            precision=EXACT,
-                            preferred_element_type=F32,
-                        )
-
+                            lower[i] = lower[i] - left[t, i, m] * lines[m]
+            return carry
+
+        lax.fori_loop(j + 1, 8, one_tile, 0)
         return carry
 
     lax.fori_loop(0, 8, one_block, 0)
@@ -283,7 +320,9 @@
         out_shape=jax.ShapeDtypeStruct((share, COLS), F32),
         scratch_shapes=[
             pltpu.VMEM((8, COLS, TILE), F32),
+            pltpu.VMEM((16, 16, 8, 8, TILE), F32),
             pltpu.VMEM((16, 8, 8, TILE), F32),
+            pltpu.VMEM((16, 8, TILE), F32),
         ],
         compiler_params=vmem(),
         name="factor",
@@ -303,22 +342,26 @@
 
 
 def all_samples(samples):
-    lines = samples
-    for axis in ("c", "y", "x", "z"):
-        lines = in_line(lines, axis)
-    return lines.transpose(2, 3, 1, 0, 4).reshape(32, -1)
+    lines = jnp.broadcast_to(samples[None, None], (32, 1, samples.shape[0]))
+    lines = lax.all_to_all(lines, PLANE, 0, 0, tiled=True)
+    return in_line(lines, "z").transpose(1, 0, 2, 3).reshape(32, -1)
 
 
 def shards(matrix, row_signs, samples):
     rows, cols = matrix.shape
     at_y, at_c = lax.axis_index("y"), lax.axis_index("c")
     at_z, at_x = lax.axis_index("z"), lax.axis_index("x")
-    flat = turned(matrix, row_signs)
-    blocks = lax.all_to_all(flat.reshape(32, 32, rows), PLANE, 0, 0, tiled=True)
     low, high = sampled_signs(at_z.reshape(1), all_samples(samples))
-    ours = picked(blocks, low, high)
-    arrived = lax.all_to_all(ours, ("z", "x"), 0, 0, tiled=True)
-    own = arrived.reshape(8, TILE, 256).sum(axis=0)
+    flats = turned(matrix, row_signs)
+    own = []
+    for n, (flat, count) in enumerate(zip(flats, CHUNKS)):
+        if n == 1:
+            flat, low, high = lax.optimization_barrier((flat, low, high))
+        blocks = lax.all_to_all(flat.reshape(32, count, rows), PLANE, 0, 0, tiled=True)
+        ours = picked(blocks, low, high)
+        arrived = lax.all_to_all(ours, ("z", "x"), 0, 0, tiled=True)
+        own.append(arrived.reshape(8, 4, count, 256).sum(axis=0))
+    own = jnp.concatenate(own, axis=1).reshape(TILE, 256)
     near, far = from_ahead(own, "y", 1), from_ahead(own, "y", 2)
     others = [from_ahead(a, "c", 1) for a in (own, near, far)]
     tiles = gram_tiles(own, near, far, *others).reshape(32, 24, TILE)

time: 348 us -> 296 us (0.85)
  Pallas kernels: 119 us -> 84.9 us
  waiting for transfers between devices: 97.5 us -> 74.5 us
  blocking collectives: 64.8 us -> 75.7 us
  starting transfers between devices: 64.5 us -> 57.5 us
    ppermute x26 -> x19, waiting for transfers between devices: 97.5 us -> 6.59 us  [from_ahead(): lax.ppermute(array, axis, [((i + shift) % size, i) for i in range(size)])]
    all_to_all x1 -> x2, waiting for transfers between devices: 0.01 us -> 67.9 us  [the longest x1 67.9 us: shards(): lax.all_to_all(flat.reshape(32, count, rows), PLANE, 0, 0, tiled=True)]
    pallas_call x1, Pallas kernels: 74.2 us -> 50.4 us  [factored(): pl.pallas_call(factor_kernel, in_specs=[pl.BlockSpec(memory_space=pltpu.S...]
    ppermute x26 -> x19, starting transfers between devices: 55.7 us -> 41.5 us  [from_ahead(): lax.ppermute(array, axis, [((i + shift) % size, i) for i in range(size)])]
    all_to_all x1, blocking collectives: 28.4 us -> 39.2 us  [shards(): arrived = lax.all_to_all(ours, ('z', 'x'), 0, 0, tiled=True)]
    pallas_call x1, Pallas kernels: 21.5 us -> 11.6 us  [picked(): pl.pallas_call(pick_kernel, grid=(2 * STEPS,), in_specs=[pl.BlockSpec((32...]
    all_to_all x1 -> x2, starting transfers between devices: 8.77 us -> 16 us  [the longest x1 8.58 us: all_samples(): lines = lax.all_to_all(lines, PLANE, 0, 0, tiled=True)]
  transfers between devices with their start and end apart: 27 -> 21, of which waited for: 11 -> 7; matrix products, arithmetic and copies ran while one was open for 0% -> 0% of each run, Pallas kernels for 4% -> 8%
where the time goes in v2:
time: 296 us; the launch traced here: 295 us
  Pallas kernels  84.9 us (29%)
  blocking collectives  75.7 us (26%)
  waiting for transfers between devices  74.5 us (25%)
  starting transfers between devices  57.5 us (19%)
    all_to_all x1, waiting for transfers between devices, shards(): lax.all_to_all(flat.reshape(32, count, rows), PLANE, 0, 0, tiled=True)  67.9 us
    pallas_call x1, Pallas kernels, factored(): pl.pallas_call(factor_kernel, in_specs=[pl.BlockSpec(memory_space=pltpu.S...  50.4 us
    ppermute x19, starting transfers between devices, from_ahead(): lax.ppermute(array, axis, [((i + shift) % size, i) for i in range(size)])  41.5 us
    all_to_all x1, blocking collectives, shards(): arrived = lax.all_to_all(ours, ('z', 'x'), 0, 0, tiled=True)  39.2 us
    all_to_all x1, blocking collectives, shards(): share = lax.all_to_all(tiles, ('z', 'x'), 0, 0, tiled=True).sum(axis=0)  18.9 us
    all_to_all x1, blocking collectives, shards(): lax.all_to_all(whole, ('z', 'x'), 0, 0, tiled=True).reshape(6, TILE, TILE)  17.6 us
    pallas_call x1, Pallas kernels, sampled_signs(): pl.pallas_call(signs_kernel, grid=(32,), in_specs=[pl.BlockSpec(memory_sp...  12.2 us
    pallas_call x1, Pallas kernels, picked(): pl.pallas_call(pick_kernel, grid=(2 * STEPS,), in_specs=[pl.BlockSpec((32...  11.6 us
  transfers between devices with their start and end apart: 21, of which 7 were waited for; matrix products, arithmetic and copies ran while one was open for 0% of the time, Pallas kernels for 8%

profile of v2, /device:TPU:1, one launch (start us, length us, event | category | flops | bytes accessed | tf_op | source)
XLA Modules:
  0.0 295.3 jit_solution(17324504171499555470)
XLA Ops:
  0.0 1.3 broadcast_in_dim.4
  1.3 8.6 %all-to-all-start.1 = ((s32[32,1,32]{2,1,0:T(1,128)}), s32[32,1,32]{2,1,0:T(1,128)S(1)}, u32[]{:S(2)}, u32[]{:S(2)}) async-start(s32[32,1,32]{2,1,0:T(1,128)} %broadcast_in_dim.4), calls=%async_computation.1 | async-start | bytes 32768 | tf_op jit(solution)/shard_map/all_to_all | solution.py:346
  9.9 0.7 copy-done
  10.6 9.9 %turn.1 = f32[1024,2048]{1,0:T(8,128)} custom-call(s32[16,128]{1,0:T(8,128)S(1)} %bitcast.46, f32[2048,1024]{1,0:T(8,128)} %in_ref.1), custom_call_target="tpu_custom_call" | custom-call | tf_op jit(solution)/shard_map/turn/pallas_call | solution.py:45
  20.5 7.4 %all-to-all-start = ((f32[32,32,2048]{2,1,0:T(8,128)}), f32[32,32,2048]{2,1,0:T(8,128)}, u32[]{:S(2)}, u32[]{:S(2)}) async-start(f32[32,32,2048]{2,1,0:T(8,128)} %bitcast.47), calls=%async_computation | async-start | bytes 16777216 | tf_op jit(solution)/shard_map/all_to_all | solution.py:360
  27.9 5.7 %collective-permute-start = (s32[32,1,32]{2,0,1:T(8,128)S(1)}, s32[32,1,32]{2,0,1:T(8,128)S(1)}, u32[]{:S(2)}, u32[]{:S(2)}) collective-permute-start(s32[32,1,32]{2,0,1:T(8,128)S(1)} %bitcast.49), channel_id=1, source_target_pairs={{8,0},{16,8},{24,16},{32,24},{40,32},{48,40},{56,48},{0,56},{9,1},... | collective-permute-start | bytes 12296 | tf_op jit(solution)/shard_map/ppermute | solution.py:334
  33.6 1.2 collective-permute-start.1
  34.8 0.4 collective-permute-start.2
  35.2 4.5 %collective-permute-start.3 = (s32[32,1,32]{2,0,1:T(8,128)S(1)}, s32[32,1,32]{2,0,1:T(8,128)S(1)}, u32[]{:S(2)}, u32[]{:S(2)}) collective-permute-start(s32[32,1,32]{2,0,1:T(8,128)S(1)} %bitcast.52), channel_id=1, source_target_pairs={{32,0},{40,8},{48,16},{56,24},{0,32},{8,40},{16,48},{24,56},{33,1}... | collective-permute-start | bytes 12296 | tf_op jit(solution)/shard_map/ppermute | solution.py:334
  39.7 2.2 collective-permute-start.5
  41.9 1.4 collective-permute-start.6
  43.3 2.4 collective-permute-done.4
  46.4 12.2 %signs.1 = (bf16[32,256,256]{2,1,0:T(8,128)(2,1)}, f32[32,8,256]{2,1,0:T(8,128)S(1)}) custom-call(s32[1]{0:T(128)} %bitcast.5.z_ref, s32[32,256]{1,0:T(8,128)S(1)} %reshape.31.sample_ref), custom_call_target="tpu_custom_call" | custom-call | tf_op jit(solution)/shard_map/signs/pallas_call | solution.py:79
  58.6 67.9 %all-to-all-done.in_ref = f32[32,32,2048]{2,1,0:T(8,128)} async-done(((f32[32,32,2048]{2,1,0:T(8,128)}), f32[32,32,2048]{2,1,0:T(8,128)}, u32[]{:S(2)}, u32[]{:S(2)}) %all-to-all-start) | async-done | bytes 8388640 | tf_op jit(solution)/shard_map/all_to_all | solution.py:360
  126.5 11.6 %pick.1 = f32[32,32,256]{2,1,0:T(8,128)S(1)} custom-call(f32[32,32,2048]{2,1,0:T(8,128)} %all-to-all-done.in_ref, bf16[32,256,256]{2,1,0:T(8,128)(2,1)} %get-tuple-element.7.low_ref, f32[32,8,256]{2,1,0:T(8,128)S(1)} %get-tuple-element.8.high_ref), custom_call_target="tpu_custom_call" | custom-call | tf_op jit(solution)/shard_map/pick/pallas_call | solution.py:152
  138.1 39.2 %all_to_all.25 = f32[32,32,256]{2,1,0:T(8,128)S(1)} all-to-all(f32[32,32,256]{2,1,0:T(8,128)S(1)} %pick.1), channel_id=1, replica_groups=mesh['x'=4,'z'=8,'y'=4,'c'=2] {'z','x'}, dimensions={0} | all-to-all | bytes 2097152 | tf_op jit(solution)/shard_map/all_to_all | solution.py:362
  177.5 1.2 collective-permute-start.8
  178.7 3.6 %collective-permute-start.9 = (f32[128,256]{1,0:T(8,128)S(1)}, f32[128,256]{1,0:T(8,128)S(1)}, u32[]{:S(2)}, u32[]{:S(2)}) collective-permute-start(f32[128,256]{1,0:T(8,128)S(1)} %bitcast.44), channel_id=1, source_target_pairs={{1,0},{0,1},{3,2},{2,3},{5,4},{4,5},{7,6},{6,7},{9,8},{8,9},{11,10... | collective-permute-start | bytes 393224 | tf_op jit(solution)/shard_map/ppermute | solution.py:334
  182.3 3.3 %collective-permute-start.10 = (f32[128,256]{1,0:T(8,128)S(1)}, f32[128,256]{1,0:T(8,128)S(1)}, u32[]{:S(2)}, u32[]{:S(2)}) collective-permute-start(f32[128,256]{1,0:T(8,128)S(1)} %collective-permute-done.7.near_ref), channel_id=1, source_target_pairs={{1,0},{0,1},{3,2},{2,3},{5,4},{4,5},{7,6},{6,7},{9,8},{8,9},{11,10... | collective-permute-start | bytes 393224 | tf_op jit(solution)/shard_map/ppermute | solution.py:334
  185.6 1.3 collective-permute-start.11
  186.9 1.0 collective-permute-done.11.o_far_ref
  187.9 0.8 gram.1
  188.7 18.9 %all_to_all.26 = f32[32,24,128]{2,1,0:T(8,128)S(1)} all-to-all(f32[32,24,128]{2,1,0:T(8,128)S(1)} %bitcast.41), channel_id=1, replica_groups=mesh['x'=4,'z'=8,'y'=4,'c'=2] {'z','x'}, dimensions={0} | all-to-all | bytes 786432 | tf_op jit(solution)/shard_map/all_to_all | solution.py:368
  207.7 17.6 %all_to_all.27 = f32[32,24,128]{2,1,0:T(8,128)S(1)} all-to-all(f32[32,24,128]{2,1,0:T(8,128)S(1)} %broadcast_in_dim.5), channel_id=1, replica_groups=mesh['x'=4,'z'=8,'y'=4,'c'=2] {'z','x'}, dimensions={0} | all-to-all | bytes 786432 | tf_op jit(solution)/shard_map/all_to_all | solution.py:370
  225.3 2.4 collective-permute-start.12
  227.8 0.7 collective-permute-start.13
  228.5 4.1 %collective-permute-start.15 = (f32[6,128,128]{2,1,0:T(8,128)S(1)}, f32[6,128,128]{2,1,0:T(8,128)S(1)}, u32[]{:S(2)}, u32[]{:S(2)}) collective-permute-start(f32[6,128,128]{2,1,0:T(8,128)S(1)} %bitcast.39), channel_id=1, source_target_pairs={{1,0},{0,1},{3,2},{2,3},{5,4},{4,5},{7,6},{6,7},{9,8},{8,9},{11,10... | collective-permute-start | bytes 1179656 | tf_op jit(solution)/shard_map/ppermute | solution.py:334
  232.6 1.7 collective-permute-done.12.refs_1_
  234.3 8.4 %collective-permute-start.16 = (f32[6,128,128]{2,1,0:T(8,128)S(1)}, f32[6,128,128]{2,1,0:T(8,128)S(1)}, u32[]{:S(2)}, u32[]{:S(2)}) collective-permute-start(f32[6,128,128]{2,1,0:T(8,128)S(1)} %collective-permute-done.12.refs_1_), channel_id=1, source_target_pairs={{1,0},{0,1},{3,2},{2,3},{5,4},{4,5},{7,6},{6,7},{9,8},{8,9},{11,10... | collective-permute-start | bytes 1179656 | tf_op jit(solution)/shard_map/ppermute | solution.py:334
  242.7 1.0 collective-permute-start.18
  243.8 0.7 collective-permute-done.17.refs_6_
  244.9 50.4 %factor.1 = f32[32,1024]{1,0:T(8,128)} custom-call(s32[3]{0:T(128)S(1)} %pad_add_fusion.at_ref, f32[6,128,128]{2,1,0:T(8,128)S(1)} %bitcast.40, f32[6,128,128]{2,1,0:T(8,128)S(1)} %collective-permute-done.12.refs_1_, f32[4,128,128]{2,1,0:T(8,128)S(1)} %collective-permute-done.13.refs_2_, f32[4,128,128]{2,1,0:T(8,128)S(1)} %collective-permute-done.14.refs_3_, ...), custom_call_target="tpu_custom_call" | custom-call | tf_op jit(solution)/shard_map/factor/pallas_call | solution.py:315
  (45 shorter events, 1.4 us)
Async XLA Ops:
  1.3 19.2 %all-to-all-start.1 = ((s32[32,1,32]{2,1,0:T(1,128)}), s32[32,1,32]{2,1,0:T(1,128)S(1)}, u32[]{:S(2)}, u32[]{:S(2)}) async-start(s32[32,1,32]{2,1,0:T(1,128)} %broadcast_in_dim.4), calls=%async_computation.1 | async-start | bytes 32768 | tf_op jit(solution)/shard_map/all_to_all | solution.py:346
  9.9 0.7 copy-start
  20.5 106.0 %all-to-all-start = ((f32[32,32,2048]{2,1,0:T(8,128)}), f32[32,32,2048]{2,1,0:T(8,128)}, u32[]{:S(2)}, u32[]{:S(2)}) async-start(f32[32,32,2048]{2,1,0:T(8,128)} %bitcast.47), calls=%async_computation | async-start | bytes 16777216 | tf_op jit(solution)/shard_map/all_to_all | solution.py:360
  27.9 11.8 %collective-permute-start = (s32[32,1,32]{2,0,1:T(8,128)S(1)}, s32[32,1,32]{2,0,1:T(8,128)S(1)}, u32[]{:S(2)}, u32[]{:S(2)}) collective-permute-start(s32[32,1,32]{2,0,1:T(8,128)S(1)} %bitcast.49), channel_id=1, source_target_pairs={{8,0},{16,8},{24,16},{32,24},{40,32},{48,40},{56,48},{0,56},{9,1},... | collective-permute-start | bytes 12296 | tf_op jit(solution)/shard_map/ppermute | solution.py:334
  33.6 8.3 %collective-permute-start.1 = (s32[32,1,32]{2,0,1:T(8,128)S(1)}, s32[32,1,32]{2,0,1:T(8,128)S(1)}, u32[]{:S(2)}, u32[]{:S(2)}) collective-permute-start(s32[32,1,32]{2,0,1:T(8,128)S(1)} %bitcast.50), channel_id=1, source_target_pairs={{16,0},{24,8},{32,16},{40,24},{48,32},{56,40},{0,48},{8,56},{17,1}... | collective-permute-start | bytes 12296 | tf_op jit(solution)/shard_map/ppermute | solution.py:334
  34.8 8.5 %collective-permute-start.2 = (s32[32,1,32]{2,0,1:T(8,128)S(1)}, s32[32,1,32]{2,0,1:T(8,128)S(1)}, u32[]{:S(2)}, u32[]{:S(2)}) collective-permute-start(s32[32,1,32]{2,0,1:T(8,128)S(1)} %bitcast.51), channel_id=1, source_target_pairs={{24,0},{32,8},{40,16},{48,24},{56,32},{0,40},{8,48},{16,56},{25,1}... | collective-permute-start | bytes 12296 | tf_op jit(solution)/shard_map/ppermute | solution.py:334
  35.2 8.0 %collective-permute-start.3 = (s32[32,1,32]{2,0,1:T(8,128)S(1)}, s32[32,1,32]{2,0,1:T(8,128)S(1)}, u32[]{:S(2)}, u32[]{:S(2)}) collective-permute-start(s32[32,1,32]{2,0,1:T(8,128)S(1)} %bitcast.52), channel_id=1, source_target_pairs={{32,0},{40,8},{48,16},{56,24},{0,32},{8,40},{16,48},{24,56},{33,1}... | collective-permute-start | bytes 12296 | tf_op jit(solution)/shard_map/ppermute | solution.py:334
  39.7 6.0 %collective-permute-start.4 = (s32[32,1,32]{2,0,1:T(8,128)S(1)}, s32[32,1,32]{2,0,1:T(8,128)S(1)}, u32[]{:S(2)}, u32[]{:S(2)}) collective-permute-start(s32[32,1,32]{2,0,1:T(8,128)S(1)} %bitcast.53), channel_id=1, source_target_pairs={{40,0},{48,8},{56,16},{0,24},{8,32},{16,40},{24,48},{32,56},{41,1}... | collective-permute-start | bytes 12296 | tf_op jit(solution)/shard_map/ppermute | solution.py:334
  39.7 6.0 %collective-permute-start.5 = (s32[32,1,32]{2,0,1:T(8,128)S(1)}, s32[32,1,32]{2,0,1:T(8,128)S(1)}, u32[]{:S(2)}, u32[]{:S(2)}) collective-permute-start(s32[32,1,32]{2,0,1:T(8,128)S(1)} %bitcast.55), channel_id=1, source_target_pairs={{48,0},{56,8},{0,16},{8,24},{16,32},{24,40},{32,48},{40,56},{49,1}... | collective-permute-start | bytes 12296 | tf_op jit(solution)/shard_map/ppermute | solution.py:334
  41.9 4.2 %collective-permute-start.6 = (s32[32,1,32]{2,1,0:T(1,128)S(1)}, s32[32,1,32]{2,1,0:T(1,128)S(1)}, u32[]{:S(2)}, u32[]{:S(2)}) collective-permute-start(s32[32,1,32]{2,1,0:T(1,128)S(1)} %all-to-all-done.1), channel_id=1, source_target_pairs={{56,0},{0,8},{8,16},{16,24},{24,32},{32,40},{40,48},{48,56},{57,1}... | collective-permute-start | bytes 12296 | tf_op jit(solution)/shard_map/ppermute | solution.py:334
  177.4 4.9 %collective-permute-start.7 = (f32[128,256]{1,0:T(8,128)S(1)}, f32[128,256]{1,0:T(8,128)S(1)}, u32[]{:S(2)}, u32[]{:S(2)}) collective-permute-start(f32[128,256]{1,0:T(8,128)S(1)} %bitcast.42), channel_id=1, source_target_pairs={{2,0},{4,2},{6,4},{0,6},{3,1},{5,3},{7,5},{1,7},{10,8},{12,10},{14... | collective-permute-start | bytes 393224 | tf_op jit(solution)/shard_map/ppermute | solution.py:334
  177.5 8.1 %collective-permute-start.8 = (f32[128,256]{1,0:T(8,128)S(1)}, f32[128,256]{1,0:T(8,128)S(1)}, u32[]{:S(2)}, u32[]{:S(2)}) collective-permute-start(f32[128,256]{1,0:T(8,128)S(1)} %bitcast.43), channel_id=1, source_target_pairs={{4,0},{6,2},{0,4},{2,6},{5,1},{7,3},{1,5},{3,7},{12,8},{14,10},{8,... | collective-permute-start | bytes 393224 | tf_op jit(solution)/shard_map/ppermute | solution.py:334
  178.7 8.2 %collective-permute-start.9 = (f32[128,256]{1,0:T(8,128)S(1)}, f32[128,256]{1,0:T(8,128)S(1)}, u32[]{:S(2)}, u32[]{:S(2)}) collective-permute-start(f32[128,256]{1,0:T(8,128)S(1)} %bitcast.44), channel_id=1, source_target_pairs={{1,0},{0,1},{3,2},{2,3},{5,4},{4,5},{7,6},{6,7},{9,8},{8,9},{11,10... | collective-permute-start | bytes 393224 | tf_op jit(solution)/shard_map/ppermute | solution.py:334
  182.3 4.6 %collective-permute-start.10 = (f32[128,256]{1,0:T(8,128)S(1)}, f32[128,256]{1,0:T(8,128)S(1)}, u32[]{:S(2)}, u32[]{:S(2)}) collective-permute-start(f32[128,256]{1,0:T(8,128)S(1)} %collective-permute-done.7.near_ref), channel_id=1, source_target_pairs={{1,0},{0,1},{3,2},{2,3},{5,4},{4,5},{7,6},{6,7},{9,8},{8,9},{11,10... | collective-permute-start | bytes 393224 | tf_op jit(solution)/shard_map/ppermute | solution.py:334
  185.6 2.3 collective-permute-start.11
  225.3 9.0 %collective-permute-start.12 = (f32[6,128,128]{2,1,0:T(8,128)S(1)}, f32[6,128,128]{2,1,0:T(8,128)S(1)}, u32[]{:S(2)}, u32[]{:S(2)}) collective-permute-start(f32[6,128,128]{2,1,0:T(8,128)S(1)} %bitcast.37), channel_id=1, source_target_pairs={{2,0},{4,2},{6,4},{0,6},{3,1},{5,3},{7,5},{1,7},{10,8},{12,10},{14... | collective-permute-start | bytes 1179656 | tf_op jit(solution)/shard_map/ppermute | solution.py:334
  227.8 15.0 %collective-permute-start.13 = (f32[4,128,128]{2,1,0:T(8,128)S(1)}, f32[4,128,128]{2,1,0:T(8,128)S(1)}, u32[]{:S(2)}, u32[]{:S(2)}) collective-permute-start(f32[4,128,128]{2,1,0:T(8,128)S(1)} %slice.5), channel_id=1, source_target_pairs={{4,0},{6,2},{0,4},{2,6},{5,1},{7,3},{1,5},{3,7},{12,8},{14,10},{8,... | collective-permute-start | bytes 786440 | tf_op jit(solution)/shard_map/ppermute | solution.py:334
  228.5 14.3 %collective-permute-start.14 = (f32[4,128,128]{2,1,0:T(8,128)S(1)}, f32[4,128,128]{2,1,0:T(8,128)S(1)}, u32[]{:S(2)}, u32[]{:S(2)}) collective-permute-start(f32[4,128,128]{2,1,0:T(8,128)S(1)} %slice.5), channel_id=1, source_target_pairs={{6,0},{0,2},{2,4},{4,6},{7,1},{1,3},{3,5},{5,7},{14,8},{8,10},{10,... | collective-permute-start | bytes 786440 | tf_op jit(solution)/shard_map/ppermute | solution.py:334
  228.5 15.3 %collective-permute-start.15 = (f32[6,128,128]{2,1,0:T(8,128)S(1)}, f32[6,128,128]{2,1,0:T(8,128)S(1)}, u32[]{:S(2)}, u32[]{:S(2)}) collective-permute-start(f32[6,128,128]{2,1,0:T(8,128)S(1)} %bitcast.39), channel_id=1, source_target_pairs={{1,0},{0,1},{3,2},{2,3},{5,4},{4,5},{7,6},{6,7},{9,8},{8,9},{11,10... | collective-permute-start | bytes 1179656 | tf_op jit(solution)/shard_map/ppermute | solution.py:334
  234.3 10.6 %collective-permute-start.16 = (f32[6,128,128]{2,1,0:T(8,128)S(1)}, f32[6,128,128]{2,1,0:T(8,128)S(1)}, u32[]{:S(2)}, u32[]{:S(2)}) collective-permute-start(f32[6,128,128]{2,1,0:T(8,128)S(1)} %collective-permute-done.12.refs_1_), channel_id=1, source_target_pairs={{1,0},{0,1},{3,2},{2,3},{5,4},{4,5},{7,6},{6,7},{9,8},{8,9},{11,10... | collective-permute-start | bytes 1179656 | tf_op jit(solution)/shard_map/ppermute | solution.py:334
  242.7 1.7 collective-permute-start.17
  242.7 2.1 collective-permute-start.18
